TPU v7x, 32 devices: a 4x4x1 block of a 4x4x8 slice. The times are simulated.
32 devices in a mesh: rep: 1 (over z), dp: 32 (over x, y, core).
Axes of the slice: x: 4, y: 4, z: 1, core: 2. Of those that a mesh axis runs over, the one named last changes fastest.
The devices are a block of a 4x4x8 slice.
Arguments:
- g_w_gate: bfloat16 [32, 2, 1024, 3200], P(('rep', 'dp'))
- g_w_up: bfloat16 [32, 2, 1024, 3200], P(('rep', 'dp'))
- g_w_down: bfloat16 [32, 2, 3200, 1024], P(('rep', 'dp'))
- w_gate: bfloat16 [2, 1024, 3200], replicated
- w_up: bfloat16 [2, 1024, 3200], replicated
- w_down: bfloat16 [2, 3200, 1024], replicated
- m_w_gate: float32 [2, 1024, 3200], P(None, 'dp')
- m_w_up: float32 [2, 1024, 3200], P(None, 'dp')
- m_w_down: float32 [2, 3200, 1024], P(None, 'dp')
- v_w_gate: float32 [2, 1024, 3200], P(None, 'dp')
- v_w_up: float32 [2, 1024, 3200], P(None, 'dp')
- v_w_down: float32 [2, 3200, 1024], P(None, 'dp')
Outputs:
- output 1: bfloat16 [2, 1024, 3200], P('rep')
- output 2: bfloat16 [2, 1024, 3200], P('rep')
- output 3: bfloat16 [2, 3200, 1024], P('rep')
- output 4: float32 [2, 1024, 3200], P('rep', 'dp')
- output 5: float32 [2, 1024, 3200], P('rep', 'dp')
- output 6: float32 [2, 3200, 1024], P('rep', 'dp')
- output 7: float32 [2, 1024, 3200], P('rep', 'dp')
- output 8: float32 [2, 1024, 3200], P('rep', 'dp')
- output 9: float32 [2, 3200, 1024], P('rep', 'dp')
All inputs are finite; a program needn't handle non-finite values.
Results may differ from a plain program's by a relative error of at most 0.022.
Values are sent between devices in bfloat16 or wider.
A program may use at most 768 MiB of HBM per device.

v0:
```python
import jax
import jax.numpy as jnp
from jax import lax
from jax.sharding import PartitionSpec as P


def adamw(w, m, v, g):
    m = 0.9 * m + 0.1 * g
    v = 0.95 * v + 0.05 * g * g
    step = m * lax.rsqrt(v + 1e-8) + 0.1 * w
    return (w - 0.02 * step).astype(jnp.bfloat16), m, v


def clipped(gradients, sum_of_squares, count):
    factor = jnp.minimum(1.0, 0.5 * lax.rsqrt(sum_of_squares / count + 1e-30))
    return [g * factor for g in gradients]


def solution(mesh):
    def step(*arrays):
        terms, weights, m, v = (arrays[i : i + 3] for i in (0, 3, 6, 9))
        gradients = [lax.psum_scatter(t[0], "dp", scatter_dimension=1, tiled=True).astype(jnp.float32) for t in terms]
        squares = lax.psum(sum(jnp.sum(g * g) for g in gradients), "dp")
        gradients = clipped(gradients, squares, lax.psum(1, "dp") * sum(g.size for g in gradients))
        me = lax.axis_index("dp")
        own = [lax.dynamic_slice_in_dim(w, me * one.shape[1], one.shape[1], 1).astype(jnp.float32) for w, one in zip(weights, m, strict=True)]
        new = [adamw(w, m, v, g) for w, m, v, g in zip(own, m, v, gradients, strict=True)]
        whole = [lax.all_gather(one[0], "dp", axis=1, tiled=True) for one in new]
        return (*whole, *(one[1] for one in new), *(one[2] for one in new))

    all_of, cut = P(None, None, None), P(None, "dp", None)
    return jax.shard_map(
        step,
        mesh=mesh,
        in_specs=(P(("rep", "dp"), None, None, None),) * 3 + (all_of,) * 3 + (cut,) * 6,
        out_specs=(P("rep", None, None),) * 3 + (P("rep", "dp", None),) * 6,
        check_vma=False,
    )
```

profile of v0, /device:TPU:97, one launch (start us, length us, event | category | flops | bytes accessed | tf_op | source)
XLA Modules:
  0.0 620.5 jit_solution(10206924068194584675)
XLA Ops:
  7.2 0.1 all-reduce.3.cloned.1.call-start
  7.3 24.6 %copy.30 = bf16[1,2,3200,1024]{3,1,2,0:T(2,128)(2,1)} copy(bf16[1,2,3200,1024]{3,2,1,0:T(8,128)(2,1)} %param.14) | data formatting | bytes 26214400 | tf_op args[2]
  31.8 0.1 all-reduce.3.cloned.1.call-update
  31.9 0.1 reduce-scatter.3.cloned.1.call-start
  32.0 0.0 copy-start.1
  32.0 0.0 copy-start.2
  32.0 0.7 reduce-scatter.3.cloned.1.call-update
  32.7 0.0 copy-start.3
  32.7 0.1 reduce-scatter.5.cloned.1.call-start
  32.8 0.7 reduce-scatter.5.cloned.1.call-update
  33.5 0.1 all-gather.8.cloned.1.call-start
  33.6 125.6 %all-reduce.3.cloned.1.call-done = bf16[2,3200,1024]{2,0,1:T(2,128)(2,1)} async-done(((bf16[2,3200,1024]{2,0,1:T(2,128)(2,1)}), bf16[2,3200,1024]{2,0,1:T(2,128)(2,1)}) %all-reduce.3.cloned.1.call-update) | async-done | bytes 13107216
  159.2 2.4 fusion.11
  161.6 97.0 %reduce-scatter.3.cloned.1.call-done = bf16[2,32,3200]{2,1,0:T(8,128)(2,1)} async-done(((bf16[2,1024,3200]{2,1,0:T(8,128)(2,1)}), bf16[2,32,3200]{2,1,0:T(8,128)(2,1)}) %reduce-scatter.3.cloned.1.call-update) | async-done | bytes 409616 | tf_op jit(solution)/shard_map/reduce_scatter | solution.py:22
  258.6 1.8 fusion.9
  260.4 99.1 %reduce-scatter.5.cloned.1.call-done = bf16[2,32,3200]{2,1,0:T(8,128)(2,1)} async-done(((bf16[2,1024,3200]{2,1,0:T(8,128)(2,1)}), bf16[2,32,3200]{2,1,0:T(8,128)(2,1)}) %reduce-scatter.5.cloned.1.call-update) | async-done | bytes 409616 | tf_op jit(solution)/shard_map/reduce_scatter | solution.py:22
  359.5 1.8 fusion.10
  363.3 1.1 constant_dynamic-slice_fusion
  364.4 46.5 %psum.7 = f32[]{:T(128)} all-reduce(f32[]{:T(128)S(6)} %add.65), channel_id=1, replica_groups=mesh['rep'=1,'dp'=32] {'dp'}, use_global_device_ids=true, to_apply=%region_6.0 | all-reduce | flops 1 | bytes 8 | tf_op jit(solution)/shard_map/psum | solution.py:23
  411.7 0.0 copy-done.1
  411.7 0.0 copy-done.2
  411.7 5.0 fusion.20
  416.7 0.1 all-gather.8.cloned.1.call-update
  416.8 0.1 all-gather.4.cloned.1.call-start
  416.9 0.0 copy-done.3
  416.9 2.9 fusion.8
  419.8 0.1 all-gather.4.cloned.1.call-update
  419.9 0.1 all-gather.6.cloned.1.call-start
  419.9 3.2 fusion.14
  423.1 0.1 all-gather.6.cloned.1.call-update
  423.1 50.9 %all-gather.8.cloned.1.call-done = bf16[2,3200,1024]{2,0,1:T(2,128)(2,1)} async-done(((bf16[2,100,1024]{2,0,1:T(2,128)(2,1)}), bf16[2,3200,1024]{2,0,1:T(2,128)(2,1)}) %all-gather.8.cloned.1.call-update) | async-done | bytes 13107216 | tf_op jit(solution)/shard_map/all_gather | solution.py:28
  474.0 12.9 %copy.26 = bf16[2,3200,1024]{2,1,0:T(8,128)(2,1)} copy(bf16[2,3200,1024]{2,0,1:T(2,128)(2,1)} %all-gather.8.cloned.1.call-done) | data formatting | bytes 26214400
  486.9 47.7 %all-gather.4.cloned.1.call-done = bf16[2,1024,3200]{2,1,0:T(8,128)(2,1)} async-done(((bf16[2,32,3200]{2,1,0:T(8,128)(2,1)}), bf16[2,1024,3200]{2,1,0:T(8,128)(2,1)}) %all-gather.4.cloned.1.call-update) | async-done | bytes 13107216 | tf_op jit(solution)/shard_map/all_gather | solution.py:28
  534.7 60.7 %all-gather.6.cloned.1.call-done = bf16[2,1024,3200]{2,1,0:T(8,128)(2,1)} async-done(((bf16[2,32,3200]{2,1,0:T(8,128)(2,1)}), bf16[2,1024,3200]{2,1,0:T(8,128)(2,1)}) %all-gather.6.cloned.1.call-update) | async-done | bytes 13107216 | tf_op jit(solution)/shard_map/all_gather | solution.py:28
  595.3 0.0 copy-start
  595.3 11.4 %copy.34 = bf16[2,1024,3200]{2,1,0:T(8,128)(2,1)} copy(bf16[2,1024,3200]{2,1,0:T(8,128)(2,1)} %all-gather.4.cloned.1.call-done) | data formatting | bytes 26214400
  606.7 2.0 copy-done
  608.7 4.9 copy.35
Async XLA Ops:
  7.2 152.0 %all-reduce.3.cloned.1.call-start = ((), (), s32[]{:S(2)}) async-start(), calls=%async_computation.7 | async-start | bytes 26214400
  31.9 226.7 %reduce-scatter.3.cloned.1.call-start = ((), (), s32[]{:S(2)}) async-start(), calls=%async_computation.2 | async-start | bytes 13516800 | tf_op jit(solution)/shard_map/reduce_scatter | solution.py:22
  32.0 379.7 %copy-start.1 = (f32[2,100,1024]{2,0,1:T(2,128)S(1)}, f32[2,100,1024]{2,0,1:T(2,128)}, u32[]{:S(2)}) copy-start(f32[2,100,1024]{2,0,1:T(2,128)} %param.23) | copy-start | bytes 2457604
  32.0 379.7 %copy-start.2 = (f32[2,100,1024]{2,0,1:T(2,128)S(1)}, f32[2,100,1024]{2,0,1:T(2,128)}, u32[]{:S(2)}) copy-start(f32[2,100,1024]{2,0,1:T(2,128)} %param.20) | copy-start | bytes 2457604
  32.7 384.2 %copy-start.3 = (f32[2,32,3200]{2,1,0:T(8,128)S(1)}, f32[2,32,3200]{2,1,0:T(8,128)}, u32[]{:S(2)}) copy-start(f32[2,32,3200]{2,1,0:T(8,128)} %param.21) | copy-start | bytes 2457604
  32.7 326.8 %reduce-scatter.5.cloned.1.call-start = ((), (), s32[]{:S(2)}) async-start(), calls=%async_computation.3 | async-start | bytes 13516800 | tf_op jit(solution)/shard_map/reduce_scatter | solution.py:22
  33.5 440.5 %all-gather.8.cloned.1.call-start = ((), (), s32[]{:S(2)}) async-start(), calls=%async_computation.6 | async-start | bytes 13516800 | tf_op jit(solution)/shard_map/all_gather | solution.py:28
  416.8 117.8 %all-gather.4.cloned.1.call-start = ((), (), s32[]{:S(2)}) async-start(), calls=%async_computation.4 | async-start | bytes 13516800 | tf_op jit(solution)/shard_map/all_gather | solution.py:28
  419.9 175.5 %all-gather.6.cloned.1.call-start = ((), (), s32[]{:S(2)}) async-start(), calls=%async_computation.5 | async-start | bytes 13516800 | tf_op jit(solution)/shard_map/all_gather | solution.py:28
  595.3 13.4 %copy-start = (bf16[2,1024,3200]{2,1,0:T(8,128)(2,1)S(1)}, bf16[2,1024,3200]{2,1,0:T(8,128)(2,1)}, u32[]{:S(2)}) copy-start(bf16[2,1024,3200]{2,1,0:T(8,128)(2,1)} %all-gather.6.cloned.1.call-done) | copy-start | bytes 39321604
Sparse Core Ops, SparseCore 0:
  32.0 127.1 all-reduce.2
  162.9 95.6 reduce-scatter.2
  262.3 97.1 reduce-scatter.4
  416.9 57.0 all-gather.7
  476.5 58.0 all-gather.3
  537.2 58.0 all-gather.5
where the time goes:
time: 621 us
  waiting for transfers between devices  483 us (78%)
  local copies, waits for them, and re-layouts  57 us (9%)
  blocking collectives  46.5 us (7%)
  other arithmetic  17.2 us (3%)
  between operations  16.9 us (3%)
    reduce_scatter x2, waiting for transfers between devices, step(): lax.psum_scatter(t[0], 'dp', scatter_dimension=1, tiled=True)  196 us
    all_gather x3, waiting for transfers between devices, step(): whole = [lax.all_gather(one[0], 'dp', axis=1, tiled=True) for one in new]  159 us
    unnamed x7, waiting for transfers between devices  127 us
    unnamed x12, local copies, waits for them, and re-layouts  55.9 us
    psum x1, blocking collectives, step(): squares = lax.psum(sum((jnp.sum(g * g) for g in gradients)), 'dp')  46.5 us
  transfers between devices with their start and end apart: 6, of which 6 were waited for; matrix products, arithmetic and copies ran while one was open for 4% of the time, Pallas kernels for 0%

commit v1 on v0

v1 whole, which is shorter than its diff:
```python
import functools
import math

import jax
import jax.numpy as jnp
from jax import lax
from jax.experimental import pallas as pl
from jax.experimental.pallas import tpu as pltpu
from jax.sharding import PartitionSpec as P

MESH = pl.DeviceIdType.MESH
CORES = 2
COLORS = 4
SLICES = 3
KEPT = COLORS // CORES
ANY = pl.BlockSpec(memory_space=pl.ANY)
VMEM = pl.BlockSpec(memory_space=pltpu.VMEM)
DMA = pltpu.SemaphoreType.DMA
ALL_VMEM = 67_043_328


def each(n, body):
    lax.fori_loop(0, n, lambda i, _: body(i), None)


class Place:
    def __init__(self, side):
        self.side = side
        self.me = lax.axis_index("dp")
        self.core = lax.rem(self.me, CORES)
        self.chip = self.me // CORES
        self.x, self.y = self.chip // side, lax.rem(self.chip, side)
        self.partner = self.me + 1 - 2 * self.core

    def at(self, x, y):
        return (x * self.side + y) * CORES + self.core

    def moved(self, p, by):
        return lax.rem(p + by + 2 * self.side, self.side)

    def way(self, q):
        on_x = q < COLORS // 2
        return jnp.where(on_x, self.x, self.y), jnp.where(on_x, self.y, self.x), 1 - 2 * lax.rem(q, 2)

    def next(self, q, first):
        up = 1 - 2 * lax.rem(q, 2)
        on_x = (q < COLORS // 2) == first
        return self.at(jnp.where(on_x, self.moved(self.x, up), self.x), jnp.where(on_x, self.y, self.moved(self.y, up)))


def remote(src, dst, send, recv, device):
    return pltpu.make_async_remote_copy(
        src_ref=src, dst_ref=dst, send_sem=send, recv_sem=recv, device_id={"dp": device}, device_id_type=MESH
    )


def part(ref, k, layer, q, t, columns):
    if k < SLICES - 1:
        return ref.at[layer, t, :, q] if q < COLORS // 2 else ref.at[layer, :, t, q]
    c = pl.ds(q * columns, columns)
    return ref.at[layer, t, :, :, c] if q < COLORS // 2 else ref.at[layer, :, t, :, c]


def wide(x):
    return x.astype(jnp.float32)


def squares(g):
    total = jnp.zeros((8, 128), jnp.float32)
    for r in range(0, g.shape[0], 8):
        for c in range(0, g.shape[1], 128):
            block = g[r : r + 8, c : c + 128]
            total += block * block
    return total


def scatter_kernel(side, n, *refs):
    terms, sums, total = refs[0:3], refs[3:6], refs[6]
    own, par, r1, r2 = refs[7:10], refs[10:13], refs[13:16], refs[16:19]
    fin, tmp, norms = refs[19:22], refs[22], refs[23]
    load, push_s, push_r, s1, v1, s2, v2, swap_s, swap_r, keep, norm_s, norm_r = refs[24:36]
    at = Place(side)
    me, core, partner = at.me, at.core, at.partner
    last = side - 1

    def group(q, s):
        p1, _, up = at.way(q)
        return at.moved(p1, -up * (1 + s))

    def loads(k, s):
        for q in range(COLORS):
            t = group(q, s)
            pltpu.make_async_copy(part(terms[k], k, core, q, t, own[k].shape[-1]), own[k].at[q, t], load.at[k, q, s]).start()

    def pushed(k, q, s, src=None):
        t = group(q, s)
        dst = par[k].at[q, t]
        return remote(dst if src is None else src, dst, push_s.at[k, q, s], push_r.at[k, q, s], partner)

    def pushes(k, s):
        for q in range(COLORS):
            pushed(k, q, s, part(terms[k], k, 1 - core, q, group(q, s), own[k].shape[-1])).start()

    def ready(k, q, s):
        t = group(q, s)
        pltpu.make_async_copy(own[k].at[q, t], own[k].at[q, t], load.at[k, q, s]).wait()
        pushed(k, q, s).wait_recv()

    def hop1(k, q, s):
        src = own[k].at[q, group(q, s)] if s == 0 else r1[k].at[q, s - 1]
        return remote(src, r1[k].at[q, s], s1.at[k, q, s], v1.at[k, q, s], at.next(q, True))

    def hop2(k, q, s):
        _, p2, up = at.way(q)
        src = r1[k].at[q, last - 1, at.moved(p2, -up)] if s == 0 else r2[k].at[q, s - 1]
        return remote(src, r2[k].at[q, s], s2.at[k, q, s], v2.at[k, q, s], at.next(q, False))

    barrier = pltpu.get_barrier_semaphore()
    each(n - 1, lambda i: pl.semaphore_signal(barrier, inc=1, device_id={"dp": lax.rem(me + 1 + i, n)}, device_id_type=MESH))
    for k in range(SLICES):
        loads(k, 0)
    pl.semaphore_wait(barrier, n - 1)
    for k in range(SLICES):
        pushes(k, 0)

    for s in range(last):
        for k in range(SLICES):

            def first(q):
                t = group(q, s)
                if s:
                    hop1(k, q, s - 1).wait_recv()
                ready(k, q, s)

                def add(j):
                    here = wide(own[k][q, t, j]) + wide(par[k][q, t, j])
                    if s:
                        r1[k][q, s - 1, j] = (wide(r1[k][q, s - 1, j]) + here).astype(jnp.bfloat16)
                    else:
                        own[k][q, t, j] = here.astype(jnp.bfloat16)

                each(side, add)
                hop1(k, q, s).start()

            each(COLORS, first)
            loads(k, s + 1)
            pushes(k, s + 1)

    def here(k, q, u):
        p1, _, _ = at.way(q)
        return wide(own[k][q, p1, u]) + wide(par[k][q, p1, u]) + wide(r1[k][q, last - 1, u])

    for s in range(last):
        for k in range(SLICES):

            def second(q):
                _, p2, up = at.way(q)
                u = at.moved(p2, -up * (1 + s))
                if s:
                    hop2(k, q, s - 1).wait_recv()
                    r2[k][q, s - 1] = (wide(r2[k][q, s - 1]) + here(k, q, u)).astype(jnp.bfloat16)
                else:
                    hop1(k, q, last - 1).wait_recv()
                    ready(k, q, last)
                    r1[k][q, last - 1, u] = here(k, q, u).astype(jnp.bfloat16)
                hop2(k, q, s).start()

            each(COLORS, second)

    norms[me] = jnp.zeros((8, 128), jnp.float32)
    for k in range(SLICES):

        def end(q):
            _, p2, _ = at.way(q)
            hop2(k, q, last - 1).wait_recv()
            g = (wide(r2[k][q, last - 1]) + here(k, q, p2)).astype(jnp.bfloat16)
            norms[me] += squares(wide(g))
            if k < SLICES - 1:
                fin[k][q] = g
            else:
                tmp[...] = wide(g)
                half = tmp.shape[0] // CORES
                for h in range(CORES):
                    fin[k][h, q] = tmp[h * half : (h + 1) * half].astype(jnp.bfloat16)

        each(COLORS, end)

    def share(k, of):
        return fin[k].at[pl.ds(of * KEPT, KEPT)] if k < SLICES - 1 else fin[k].at[of]

    def norm(i):
        return remote(norms.at[me], norms.at[me], norm_s.at[i], norm_r.at[i], lax.rem(me + 1 + i, n))

    each(n - 1, lambda i: norm(i).start())
    swaps = [remote(share(k, 1 - core), sums[k].at[core], swap_s.at[k], swap_r.at[k], partner) for k in range(SLICES)]
    keeps = [pltpu.make_async_copy(share(k, core), sums[k].at[core], keep.at[k]) for k in range(SLICES)]
    for copy in swaps + keeps:
        copy.start()
    each(n - 1, lambda i: norm(i).wait_recv())
    total[...] = jnp.zeros((8, 128), jnp.float32)

    def tally(i):
        total[...] += norms[i]

    each(n, tally)
    each(n - 1, lambda i: norm(i).wait_send())
    for copy in keeps:
        copy.wait()
    for k in range(SLICES):
        remote(share(k, 1 - core), sums[k].at[1 - core], swap_s.at[k], swap_r.at[k], partner).wait_recv()
        swaps[k].wait_send()

        def drain(q):
            for s in range(side):
                pushed(k, q, s).wait_send()
            for s in range(last):
                hop1(k, q, s).wait_send()
                hop2(k, q, s).wait_send()

        each(COLORS, drain)


def factor_of(total, count):
    return jnp.minimum(1.0, 0.5 * lax.rsqrt(jnp.sum(total) / count + 1e-30))


def moments(m, v, g):
    return 0.9 * m + 0.1 * g, 0.95 * v + 0.05 * g * g


def new_weight(w, m, v, g):
    m, v = moments(m, v, g)
    return (w - 0.02 * (m * lax.rsqrt(v + 1e-8) + 0.1 * w)).astype(jnp.bfloat16)


def lanes_of(layers, rows, q, columns, layer):
    per_row = COLORS * columns // 128 * layers
    return [pl.ds((q * columns // 128 + i) * layers + layer, rows, stride=per_row) for i in range(columns // 128)]


def gather_kernel(side, count, *refs):
    total, sums, weights, m, v = refs[0], refs[1:4], refs[4:7], refs[7:10], refs[10:13]
    out = refs[13:16]
    gb, wb, mb, vb = refs[16:19], refs[19:22], refs[22:25], refs[25:28]
    half_w, tmp, lent = refs[28], refs[29], refs[30:32]
    load, swap_s, swap_r, s1, v1, s2, v2, push_s, push_r = refs[32:41]
    at = Place(side)
    me, core, partner = at.me, at.core, at.partner
    other = 1 - core
    last = side - 1
    down = SLICES - 1

    barrier = pltpu.get_barrier_semaphore()
    near = [partner] + [at.next(q, True) for q in range(COLORS)]
    for device in near:
        pl.semaphore_signal(barrier, inc=1, device_id={"dp": device}, device_id_type=MESH)
    sources = [[sums[k], weights[k].at[:, me if k < down else at.chip], m[k], v[k]] for k in range(SLICES)]
    copies = [
        [pltpu.make_async_copy(src, dst[k], load.at[k, i]) for i, (src, dst) in enumerate(zip(sources[k], (gb, wb, mb, vb), strict=True))]
        for k in range(SLICES)
    ]
    for copy in sum(copies, []):
        copy.start()
    pl.semaphore_wait(barrier, len(near))
    factor = factor_of(total[...], count)

    def mine(k, layer, q):
        p1, p2, _ = at.way(q)
        return out[k].at[layer, q, p1, p2]

    def swap(k, i, q, layer):
        return remote(lent[k].at[i], mine(k, layer, q), swap_s.at[k, i], swap_r.at[k, i], partner)

    def hop1(k, q, s):
        p1, p2, up = at.way(q)
        ref = out[k].at[core, q, p1, at.moved(p2, -up * s)]
        return remote(ref, ref, s1.at[k, q, s], v1.at[k, q, s], at.next(q, False))

    def hop2(k, q, s):
        p1, _, up = at.way(q)
        ref = out[k].at[core, q, at.moved(p1, -up * s)]
        return remote(ref, ref, s2.at[k, q, s], v2.at[k, q, s], at.next(q, True))

    def push(k, q, s, layer):
        p1, _, up = at.way(q)
        ref = out[k].at[layer, q, at.moved(p1, -up * s)]
        return remote(ref, ref, push_s.at[k, q, s], push_r.at[k, q, s], partner)

    for k in range(down):
        for copy in copies[k]:
            copy.wait()
        for layer in (other, core):
            for i in range(KEPT):
                p1, p2, _ = at.way(core * KEPT + i)
                w = new_weight(wide(wb[k][layer, i]), mb[k][layer, i], vb[k][layer, i], wide(gb[k][layer, i]) * factor)
                if layer is other:
                    lent[k][i] = w
                    swap(k, i, core * KEPT + i, other).start()
                else:
                    out[k][layer, core * KEPT + i, p1, p2] = w

    for copy in copies[down]:
        copy.wait()
    rows, columns = half_w.shape[-2:]
    half_swap = remote(half_w.at[1], half_w.at[2], swap_s.at[down, 0], swap_r.at[down, 0], partner)
    for slot in (1, 0):
        for layer in range(CORES):

            @pl.when((layer == core) == (slot == 0))
            def _(layer=layer, slot=slot):
                for q in range(COLORS):
                    tmp[...] = wide(wb[down][layer, :, q * columns : (q + 1) * columns])
                    start = lax.select(core == 0, 0, 1)
                    w = jnp.where(start == 0, tmp[0:rows], tmp[rows : 2 * rows])
                    where = lanes_of(CORES, rows, q, columns, layer)
                    one = jnp.concatenate([mb[down][i, :] for i in where], axis=1)
                    two = jnp.concatenate([vb[down][i, :] for i in where], axis=1)
                    half_w[slot, q] = new_weight(w, one, two, wide(gb[down][layer, q]) * factor)

        if slot:
            half_swap.start()

    for k in range(down):
        for i in range(KEPT):
            swap(k, i, other * KEPT + i, core).wait_recv()

        each(COLORS, lambda q, k=k: hop1(k, q, 0).start())
    half_swap.wait_recv()
    top = 2 * core
    for q in range(COLORS):
        p1, p2, _ = at.way(q)
        tmp[0:rows] = wide(half_w[top, q])
        tmp[rows : 2 * rows] = wide(half_w[2 - top, q])
        out[down][core, q, p1, p2] = tmp[...].astype(jnp.bfloat16)
        hop1(down, q, 0).start()

    for s in range(1, last):
        for k in range(SLICES):

            def first(q):
                hop1(k, q, s - 1).wait_recv()
                hop1(k, q, s).start()

            each(COLORS, first)
    for s in range(side):
        for k in range(SLICES):

            def second(q):
                if s:
                    hop2(k, q, s - 1).wait_recv()
                else:
                    hop1(k, q, last - 1).wait_recv()
                if s < last:
                    hop2(k, q, s).start()
                push(k, q, s, core).start()

            each(COLORS, second)

    for k in range(SLICES):

        def drain(q):
            for s in range(side):
                push(k, q, s, other).wait_recv()
                push(k, q, s, core).wait_send()
            for s in range(last):
                hop1(k, q, s).wait_send()
                hop2(k, q, s).wait_send()

        each(COLORS, drain)
        if k < down:
            for i in range(KEPT):
                swap(k, i, core * KEPT + i, other).wait_send()
    half_swap.wait_send()


def finish_kernel(side, count, *refs):
    whole, total, sums, m, v = refs[0:3], refs[3], refs[4:7], refs[7:10], refs[10:13]
    new, new_m, new_v = refs[13:16], refs[16:19], refs[19:22]
    gb, mb, vb = refs[22:25], refs[25:28], refs[28:31]
    write, load, store = refs[31:34]
    down = SLICES - 1
    copies = [
        [pltpu.make_async_copy(src[k], dst[k], load.at[k, i]) for i, (src, dst) in enumerate(((sums, gb), (m, mb), (v, vb)))]
        for k in range(SLICES)
    ]
    for copy in sum(copies, []):
        copy.start()
    for k in range(SLICES):
        for layer in range(CORES):
            for q in range(COLORS):

                def put(t, k=k, layer=layer, q=q):
                    pltpu.make_async_copy(
                        whole[k].at[layer, q, t], part(new[k], k, layer, q, t, whole[k].shape[-1]), write.at[k, layer, q, t]
                    ).start()

                each(side, put)
    factor = factor_of(total[...], count)
    for k in range(SLICES):
        for copy in copies[k]:
            copy.wait()
        for layer in range(CORES):
            if k < down:
                for i in range(KEPT):
                    one, two = moments(mb[k][layer, i], vb[k][layer, i], wide(gb[k][layer, i]) * factor)
                    mb[k][layer, i] = one
                    vb[k][layer, i] = two
            else:
                rows, columns = gb[k].shape[-2:]
                for q in range(COLORS):
                    g = wide(gb[k][layer, q]) * factor
                    for i, where in enumerate(lanes_of(CORES, rows, q, columns, layer)):
                        one, two = moments(mb[k][where, :], vb[k][where, :], g[:, i * 128 : (i + 1) * 128])
                        mb[k][where, :] = one
                        vb[k][where, :] = two
        pltpu.make_async_copy(mb[k], new_m[k], store.at[k, 0]).start()
        pltpu.make_async_copy(vb[k], new_v[k], store.at[k, 1]).start()
    for k in range(SLICES):
        pltpu.make_async_copy(mb[k], new_m[k], store.at[k, 0]).wait()
        pltpu.make_async_copy(vb[k], new_v[k], store.at[k, 1]).wait()
        for layer in range(CORES):

            def wrote(i, k=k, layer=layer):
                q, t = i // side, lax.rem(i, side)
                pltpu.make_async_copy(whole[k].at[layer, q, t], whole[k].at[layer, q, t], write.at[k, layer, q, t]).wait()

            each(COLORS * side, wrote)


def solution(mesh):
    n = mesh.shape["dp"]
    side = math.isqrt(n // CORES)
    bf16, f32 = jnp.bfloat16, jnp.float32
    shape = jax.ShapeDtypeStruct

    def step(*arrays):
        terms, weights, m, v = (arrays[i : i + 3] for i in (0, 3, 6, 9))
        layers, depth, wide_columns = weights[0].shape
        _, deep, columns = weights[2].shape
        chips = side * side
        high, tall = depth // chips // COLORS, deep // chips
        pieces = [(high, wide_columns)] * 2 + [(tall, columns // COLORS)]
        half = (COLORS, tall // CORES, columns // COLORS)
        count = sum(w.size for w in weights)

        views = [t.reshape(layers, side, side, COLORS, high, wide_columns) for t in terms[:2]]
        views.append(terms[2].reshape(layers, side, side, tall, columns))
        kept = [shape((layers, KEPT, high, wide_columns), bf16)] * 2 + [shape((layers, *half), bf16)]
        *sums, total = pl.pallas_call(
            functools.partial(scatter_kernel, side, n),
            name="scatter",
            out_shape=(*kept, shape((8, 128), f32)),
            in_specs=[ANY] * 3,
            out_specs=(ANY,) * 3 + (VMEM,),
            scratch_shapes=[
                *(pltpu.VMEM((COLORS, side, side, *p), bf16) for p in pieces),
                *(pltpu.VMEM((COLORS, side, side, *p), bf16) for p in pieces),
                *(pltpu.VMEM((COLORS, side - 1, side, *p), bf16) for p in pieces),
                *(pltpu.VMEM((COLORS, side - 1, *p), bf16) for p in pieces),
                *(pltpu.VMEM((COLORS, *p), bf16) for p in pieces[:2]),
                pltpu.VMEM((CORES, *half), bf16),
                pltpu.VMEM(pieces[2], f32),
                pltpu.VMEM((n, 8, 128), f32),
                *(DMA((SLICES, COLORS, side)) for _ in range(3)),
                *(DMA((SLICES, COLORS, side - 1)) for _ in range(4)),
                *(DMA((SLICES,)) for _ in range(3)),
                *(DMA((n - 1,)) for _ in range(2)),
            ],
            compiler_params=pltpu.CompilerParams(collective_id=0, has_side_effects=True, vmem_limit_bytes=ALL_VMEM),
        )(*views)

        def by_lanes(a):
            layers, rows, columns = a.shape
            a = a.transpose(1, 0, 2).reshape(rows, layers, columns // 128, 128)
            return a.transpose(0, 2, 1, 3).reshape(-1, 128)

        def by_rows(a, like):
            layers, rows, columns = like.shape
            a = a.reshape(rows, columns // 128, layers, 128).transpose(0, 2, 1, 3)
            return a.reshape(rows, layers, columns).transpose(1, 0, 2)

        own = [w.reshape(layers, n, KEPT, high, wide_columns) for w in weights[:2]]
        own.append(weights[2].reshape(layers, chips, tall, columns))
        ms, vs = ([a.reshape(layers, KEPT, high, wide_columns) for a in b[:2]] + [by_lanes(b[2])] for b in (m, v))
        state = [pltpu.VMEM(a.shape, f32) for a in ms]
        gathered = pl.pallas_call(
            functools.partial(gather_kernel, side, count),
            name="gather",
            out_shape=tuple(pltpu.VMEM((layers, COLORS, side, side, *p), bf16) for p in pieces),
            in_specs=[VMEM] + [ANY] * 12,
            out_specs=(VMEM,) * 3,
            scratch_shapes=[
                *(pltpu.VMEM(k.shape, bf16) for k in kept),
                *(pltpu.VMEM((layers, KEPT, high, wide_columns), bf16) for _ in range(2)),
                pltpu.VMEM((layers, tall, columns), bf16),
                *state,
                *state,
                pltpu.VMEM((CORES + 1, *half), bf16),
                pltpu.VMEM(pieces[2], f32),
                *(pltpu.VMEM((KEPT, *p), bf16) for p in pieces[:2]),
                DMA((SLICES, 4)),
                *(DMA((SLICES, KEPT)) for _ in range(2)),
                *(DMA((SLICES, COLORS, side - 1)) for _ in range(4)),
                *(DMA((SLICES, COLORS, side)) for _ in range(2)),
            ],
            compiler_params=pltpu.CompilerParams(collective_id=1, has_side_effects=True, vmem_limit_bytes=20 << 20),
        )(total, *sums, *own, *ms, *vs)

        gathered = [pltpu.with_memory_space_constraint(a, pltpu.VMEM) for a in gathered]
        outs = pl.pallas_call(
            functools.partial(finish_kernel, side, count),
            name="finish",
            out_shape=tuple(shape(a.shape, a.dtype) for a in (*[shape(t.shape, bf16) for t in views], *ms, *vs)),
            in_specs=[VMEM] * 4 + [ANY] * 9,
            out_specs=(ANY,) * 9,
            scratch_shapes=[
                *(pltpu.VMEM(k.shape, bf16) for k in kept),
                *state,
                *state,
                DMA((SLICES, CORES, COLORS, side)),
                DMA((SLICES, 3)),
                DMA((SLICES, 2)),
            ],
            compiler_params=pltpu.CompilerParams(vmem_limit_bytes=20 << 20),
        )(*gathered, total, *sums, *ms, *vs)
        new = [a.reshape(w.shape) for a, w in zip(outs[:3], weights, strict=True)]
        rest = [
            (by_rows(a, like) if i == SLICES - 1 else a.reshape(like.shape))
            for block in (outs[3:6], outs[6:9])
            for i, (a, like) in enumerate(zip(block, m, strict=True))
        ]
        return (*new, *rest)

    all_of, cut = P(None, None, None), P(None, "dp", None)
    return jax.shard_map(
        step,
        mesh=mesh,
        in_specs=(P(("rep", "dp"), None, None, None),) * 3 + (all_of,) * 3 + (cut,) * 6,
        out_specs=(P("rep", None, None),) * 3 + (P("rep", "dp", None),) * 6,
        check_vma=False,
    )
```

time: 621 us -> 254 us (0.41)
  waiting for transfers between devices: 483 us -> 0 us
  Pallas kernels: 0 us -> 253 us
  local copies, waits for them, and re-layouts: 57 us -> 0 us
  blocking collectives: 46.5 us -> 0 us
  other arithmetic: 17.2 us -> 0 us
  between operations: 16.9 us -> 0.66 us
    pallas_call x0 -> x3, Pallas kernels: none -> 253 us  [the longest x1 123 us: step(): pl.pallas_call(functools.partial(scatter_kernel, side, n), name='scatter'...]
    reduce_scatter x2 -> x0, waiting for transfers between devices: 196 us -> none  [step(): lax.psum_scatter(t[0], 'dp', scatter_dimension=1, tiled=True)]
    all_gather x3 -> x0, waiting for transfers between devices: 159 us -> none  [step(): whole = [lax.all_gather(one[0], 'dp', axis=1, tiled=True) for one in new]]
    unnamed x7 -> x0, waiting for transfers between devices: 127 us -> none
    unnamed x12 -> x0, local copies, waits for them, and re-layouts: 55.9 us -> none
    psum x1 -> x0, blocking collectives: 46.5 us -> none  [step(): squares = lax.psum(sum((jnp.sum(g * g) for g in gradients)), 'dp')]
    convert_element_type x3 -> x0, other arithmetic: 11.1 us -> none  [adamw(): return ((w - 0.02 * step).astype(jnp.bfloat16), m, v)]
  transfers between devices with their start and end apart: 6 -> 0, of which waited for: 6 -> 0; matrix products, arithmetic and copies ran while one was open for 4% -> 0% of each run, Pallas kernels for 0% -> 0%
where the time goes in v1:
time: 254 us
  Pallas kernels  253 us (100%)
    pallas_call x1, Pallas kernels, step(): pl.pallas_call(functools.partial(scatter_kernel, side, n), name='scatter'...  123 us
    pallas_call x1, Pallas kernels, step(): pl.pallas_call(functools.partial(gather_kernel, side, count), name='gathe...  113 us
    pallas_call x1, Pallas kernels, step(): pl.pallas_call(functools.partial(finish_kernel, side, count), name='finis...  17.7 us

profile of v1, /device:TPU:97, one launch (start us, length us, event | category | flops | bytes accessed | tf_op | source)
XLA Modules:
  0.0 254.1 jit_solution(14437760400928080742)
XLA Ops:
  0.6 123.1 %scatter.1 = (bf16[2,2,16,3200]{3,2,1,0:T(8,128)(2,1)}, bf16[2,2,16,3200]{3,2,1,0:T(8,128)(2,1)}, bf16[2,4,100,256]{3,2,1,0:T(8,128)(2,1)}, f32[8,128]{1,0:T(8,128)}) custom-call(bf16[2,4,4,4,16,3200]{5,4,3,2,1,0:T(8,128)(2,1)} %bitcast.45, bf16[2,4,4,4,16,3200]{5,4,3,2,1,0:T(8,128)(2,1)} %bitcast.46, bf16[2,4,4,200,1024]{4,3,2,1,0:T(8,128)(2,1)} %bitcast.47), custom_call_target="tpu_custom_call" | custom-call | tf_op jit(solution)/shard_map/scatter/pallas_call | solution.py:449
  123.7 112.7 %gather.1 = (bf16[2,4,4,4,16,3200]{5,4,3,2,1,0:T(8,128)(2,1)S(1)}, bf16[2,4,4,4,16,3200]{5,4,3,2,1,0:T(8,128)(2,1)S(1)}, bf16[2,4,4,4,200,256]{5,4,3,2,1,0:T(8,128)(2,1)S(1)}) custom-call(f32[8,128]{1,0:T(8,128)} %get-tuple-element.25.refs_0_.refs_3_, bf16[2,2,16,3200]{3,2,1,0:T(8,128)(2,1)} %get-tuple-element.26.refs_1_.refs_4_, ...), custom_call_target="tpu_custom_call" | custom-call | tf_op jit(solution)/shard_map/gather/pallas_call | solution.py:486
  236.5 17.7 %finish.1 = (bf16[2,4,4,4,16,3200]{5,4,3,2,1,0:T(8,128)(2,1)}, bf16[2,4,4,4,16,3200]{5,4,3,2,1,0:T(8,128)(2,1)}, bf16[2,4,4,200,1024]{4,3,2,1,0:T(8,128)(2,1)}, ...) custom-call(bf16[2,4,4,4,16,3200]{5,4,3,2,1,0:T(8,128)(2,1)S(1)} %ge, ...), custom_call_target="tpu_custom_call" | custom-call | tf_op jit(solution)/shard_map/finish/pallas_call | solution.py:510

commit v2 on v1

--- a/solution.py
+++ b/solution.py
@@ -54,6 +54,14 @@
     )
 
 
+def meet(at):
+    barrier = pltpu.get_barrier_semaphore()
+    near = [at.partner] + [at.next(q, True) for q in range(COLORS)]
+    for device in near:
+        pl.semaphore_signal(barrier, inc=1, device_id={"dp": device}, device_id_type=MESH)
+    return lambda: pl.semaphore_wait(barrier, len(near))
+
+
 def part(ref, k, layer, q, t, columns):
     if k < SLICES - 1:
         return ref.at[layer, t, :, q] if q < COLORS // 2 else ref.at[layer, :, t, q]
@@ -79,6 +87,7 @@
     own, par, r1, r2 = refs[7:10], refs[10:13], refs[13:16], refs[16:19]
     fin, tmp, norms = refs[19:22], refs[22], refs[23]
     load, push_s, push_r, s1, v1, s2, v2, swap_s, swap_r, keep, norm_s, norm_r = refs[24:36]
+    piece_s, piece_r, s1_piece, v1_piece = refs[36:40]
     at = Place(side)
     me, core, partner = at.me, at.core, at.partner
     last = side - 1
@@ -101,9 +110,12 @@
         for q in range(COLORS):
             pushed(k, q, s, part(terms[k], k, 1 - core, q, group(q, s), own[k].shape[-1])).start()
 
-    def ready(k, q, s):
+    def loaded(k, q, s):
         t = group(q, s)
         pltpu.make_async_copy(own[k].at[q, t], own[k].at[q, t], load.at[k, q, s]).wait()
+
+    def ready(k, q, s):
+        loaded(k, q, s)
         pushed(k, q, s).wait_recv()
 
     def hop1(k, q, s):
@@ -115,20 +127,46 @@
         src = r1[k].at[q, last - 1, at.moved(p2, -up)] if s == 0 else r2[k].at[q, s - 1]
         return remote(src, r2[k].at[q, s], s2.at[k, q, s], v2.at[k, q, s], at.next(q, False))
 
-    barrier = pltpu.get_barrier_semaphore()
-    each(n - 1, lambda i: pl.semaphore_signal(barrier, inc=1, device_id={"dp": lax.rem(me + 1 + i, n)}, device_id_type=MESH))
+    def pushed_piece(q, j, src=None):
+        dst = par[0].at[q, group(q, 0), j]
+        return remote(dst if src is None else src, dst, piece_s.at[q, j], piece_r.at[q, j], partner)
+
+    def hop1_piece(q, j):
+        return remote(own[0].at[q, group(q, 0), j], r1[0].at[q, 0, j], s1_piece.at[q, j], v1_piece.at[q, j], at.next(q, True))
+
+    greet = meet(at)
     for k in range(SLICES):
         loads(k, 0)
-    pl.semaphore_wait(barrier, n - 1)
-    for k in range(SLICES):
+    greet()
+    for j in range(side):
+        for q in range(COLORS):
+            pushed_piece(q, j, part(terms[0], 0, 1 - core, q, group(q, 0), own[0].shape[-1]).at[j]).start()
+    for k in range(1, SLICES):
         pushes(k, 0)
+    for j in range(side):
+
+        def start(q):
+            t = group(q, 0)
+            if j == 0:
+                loaded(0, q, 0)
+            pushed_piece(q, j).wait_recv()
+            own[0][q, t, j] = (wide(own[0][q, t, j]) + wide(par[0][q, t, j])).astype(jnp.bfloat16)
+            hop1_piece(q, j).start()
+
+        each(COLORS, start)
+    loads(0, 1)
+    pushes(0, 1)
 
     for s in range(last):
         for k in range(SLICES):
+            if s == 0 and k == 0:
+                continue
 
             def first(q):
                 t = group(q, s)
-                if s:
+                if s == 1 and k == 0:
+                    each(side, lambda j: hop1_piece(q, j).wait_recv())
+                elif s:
                     hop1(k, q, s - 1).wait_recv()
                 ready(k, q, s)
 
@@ -211,11 +249,20 @@
         swaps[k].wait_send()
 
         def drain(q):
-            for s in range(side):
+            whole_from = 1 if k == 0 else 0
+            for s in range(whole_from, side):
                 pushed(k, q, s).wait_send()
             for s in range(last):
-                hop1(k, q, s).wait_send()
+                if s >= whole_from:
+                    hop1(k, q, s).wait_send()
                 hop2(k, q, s).wait_send()
+            if whole_from:
+
+                def pieces(j):
+                    pushed_piece(q, j).wait_send()
+                    hop1_piece(q, j).wait_send()
+
+                each(side, pieces)
 
         each(COLORS, drain)
 
@@ -240,20 +287,18 @@
 
 def gather_kernel(side, count, *refs):
     total, sums, weights, m, v = refs[0], refs[1:4], refs[4:7], refs[7:10], refs[10:13]
-    out = refs[13:16]
-    gb, wb, mb, vb = refs[16:19], refs[19:22], refs[22:25], refs[25:28]
+    out, mb, vb = refs[13:16], refs[16:19], refs[19:22]
+    gb, wb = refs[22:25], refs[25:28]
     half_w, tmp, lent = refs[28], refs[29], refs[30:32]
     load, swap_s, swap_r, s1, v1, s2, v2, push_s, push_r = refs[32:41]
+    s2_piece, v2_piece, piece_s, piece_r = refs[41:45]
     at = Place(side)
     me, core, partner = at.me, at.core, at.partner
     other = 1 - core
     last = side - 1
     down = SLICES - 1
 
-    barrier = pltpu.get_barrier_semaphore()
-    near = [partner] + [at.next(q, True) for q in range(COLORS)]
-    for device in near:
-        pl.semaphore_signal(barrier, inc=1, device_id={"dp": device}, device_id_type=MESH)
+    greet = meet(at)
     sources = [[sums[k], weights[k].at[:, me if k < down else at.chip], m[k], v[k]] for k in range(SLICES)]
     copies = [
         [pltpu.make_async_copy(src, dst[k], load.at[k, i]) for i, (src, dst) in enumerate(zip(sources[k], (gb, wb, mb, vb), strict=True))]
@@ -261,7 +306,7 @@
     ]
     for copy in sum(copies, []):
         copy.start()
-    pl.semaphore_wait(barrier, len(near))
+    greet()
     factor = factor_of(total[...], count)
 
     def mine(k, layer, q):
@@ -286,45 +331,77 @@
         ref = out[k].at[layer, q, at.moved(p1, -up * s)]
         return remote(ref, ref, push_s.at[k, q, s], push_r.at[k, q, s], partner)
 
-    for k in range(down):
+    def hop2_piece(q, j):
+        p1, _, up = at.way(q)
+        ref = out[down].at[core, q, at.moved(p1, -up * (last - 1)), j]
+        return remote(ref, ref, s2_piece.at[q, j], v2_piece.at[q, j], at.next(q, True))
+
+    def push_piece(q, j, layer):
+        p1, _, up = at.way(q)
+        ref = out[down].at[layer, q, at.moved(p1, -up * last), j]
+        return remote(ref, ref, piece_s.at[q, j], piece_r.at[q, j], partner)
+
+    def step(k):
         for copy in copies[k]:
             copy.wait()
         for layer in (other, core):
             for i in range(KEPT):
-                p1, p2, _ = at.way(core * KEPT + i)
+                q = core * KEPT + i
                 w = new_weight(wide(wb[k][layer, i]), mb[k][layer, i], vb[k][layer, i], wide(gb[k][layer, i]) * factor)
                 if layer is other:
                     lent[k][i] = w
-                    swap(k, i, core * KEPT + i, other).start()
+                    swap(k, i, q, other).start()
                 else:
-                    out[k][layer, core * KEPT + i, p1, p2] = w
-
-    for copy in copies[down]:
-        copy.wait()
+                    p1, p2, _ = at.way(q)
+                    out[k][layer, q, p1, p2] = w
+                    hop1(k, q, 0).start()
+
+    def swapped(k):
+        for i in range(KEPT):
+            q = other * KEPT + i
+            swap(k, i, q, core).wait_recv()
+            hop1(k, q, 0).start()
+
     rows, columns = half_w.shape[-2:]
     half_swap = remote(half_w.at[1], half_w.at[2], swap_s.at[down, 0], swap_r.at[down, 0], partner)
-    for slot in (1, 0):
+
+    def step_down(slot):
         for layer in range(CORES):
 
             @pl.when((layer == core) == (slot == 0))
-            def _(layer=layer, slot=slot):
+            def _(layer=layer):
                 for q in range(COLORS):
                     tmp[...] = wide(wb[down][layer, :, q * columns : (q + 1) * columns])
-                    start = lax.select(core == 0, 0, 1)
-                    w = jnp.where(start == 0, tmp[0:rows], tmp[rows : 2 * rows])
+                    w = jnp.where(core == 0, tmp[0:rows], tmp[rows : 2 * rows])
                     where = lanes_of(CORES, rows, q, columns, layer)
                     one = jnp.concatenate([mb[down][i, :] for i in where], axis=1)
                     two = jnp.concatenate([vb[down][i, :] for i in where], axis=1)
                     half_w[slot, q] = new_weight(w, one, two, wide(gb[down][layer, q]) * factor)
 
-        if slot:
-            half_swap.start()
-
-    for k in range(down):
-        for i in range(KEPT):
-            swap(k, i, other * KEPT + i, core).wait_recv()
-
-        each(COLORS, lambda q, k=k: hop1(k, q, 0).start())
+    def keep_moments(k):
+        for layer in range(CORES):
+            if k < down:
+                for i in range(KEPT):
+                    one, two = moments(mb[k][layer, i], vb[k][layer, i], wide(gb[k][layer, i]) * factor)
+                    mb[k][layer, i] = one
+                    vb[k][layer, i] = two
+            else:
+                for q in range(COLORS):
+                    g = wide(gb[k][layer, q]) * factor
+                    for i, where in enumerate(lanes_of(CORES, rows, q, columns, layer)):
+                        one, two = moments(mb[k][where, :], vb[k][where, :], g[:, i * 128 : (i + 1) * 128])
+                        mb[k][where, :] = one
+                        vb[k][where, :] = two
+
+    step(0)
+    step(1)
+    swapped(0)
+    for copy in copies[down]:
+        copy.wait()
+    step_down(1)
+    half_swap.start()
+    swapped(1)
+    step_down(0)
     half_swap.wait_recv()
     top = 2 * core
     for q in range(COLORS):
@@ -350,21 +427,44 @@
                     hop2(k, q, s - 1).wait_recv()
                 else:
                     hop1(k, q, last - 1).wait_recv()
-                if s < last:
+                if k == down and s == last - 1:
+                    each(side, lambda j: hop2_piece(q, j).start())
+                elif s < last:
                     hop2(k, q, s).start()
                 push(k, q, s, core).start()
 
-            each(COLORS, second)
+            if k == down and s == last:
+
+                def end(i):
+                    j, q = i // COLORS, lax.rem(i, COLORS)
+                    hop2_piece(q, j).wait_recv()
+                    push_piece(q, j, core).start()
+
+                each(side * COLORS, end)
+            else:
+                each(COLORS, second)
+            if s == 0:
+                keep_moments(k)
 
     for k in range(SLICES):
 
         def drain(q):
-            for s in range(side):
+            cut = 1 if k == down else 0
+            for s in range(side - cut):
                 push(k, q, s, other).wait_recv()
                 push(k, q, s, core).wait_send()
             for s in range(last):
                 hop1(k, q, s).wait_send()
-                hop2(k, q, s).wait_send()
+                if s < last - cut:
+                    hop2(k, q, s).wait_send()
+            if cut:
+
+                def pieces(j):
+                    push_piece(q, j, other).wait_recv()
+                    push_piece(q, j, core).wait_send()
+                    hop2_piece(q, j).wait_send()
+
+                each(side, pieces)
 
         each(COLORS, drain)
         if k < down:
@@ -373,51 +473,23 @@
     half_swap.wait_send()
 
 
-def finish_kernel(side, count, *refs):
-    whole, total, sums, m, v = refs[0:3], refs[3], refs[4:7], refs[7:10], refs[10:13]
-    new, new_m, new_v = refs[13:16], refs[16:19], refs[19:22]
-    gb, mb, vb = refs[22:25], refs[25:28], refs[28:31]
-    write, load, store = refs[31:34]
-    down = SLICES - 1
-    copies = [
-        [pltpu.make_async_copy(src[k], dst[k], load.at[k, i]) for i, (src, dst) in enumerate(((sums, gb), (m, mb), (v, vb)))]
-        for k in range(SLICES)
-    ]
-    for copy in sum(copies, []):
-        copy.start()
+def finish_kernel(side, *refs):
+    whole, state, new, new_state, write, store = refs[0:3], refs[3:9], refs[9:12], refs[12:18], refs[18], refs[19]
     for k in range(SLICES):
         for layer in range(CORES):
             for q in range(COLORS):
 
                 def put(t, k=k, layer=layer, q=q):
-                    pltpu.make_async_copy(
-                        whole[k].at[layer, q, t], part(new[k], k, layer, q, t, whole[k].shape[-1]), write.at[k, layer, q, t]
-                    ).start()
+                    src, dst = whole[k].at[layer, q, t], part(new[k], k, layer, q, t, whole[k].shape[-1])
+                    pltpu.make_async_copy(src, dst, write.at[k, layer, q, t]).start()
 
                 each(side, put)
-    factor = factor_of(total[...], count)
+    copies = [pltpu.make_async_copy(src, dst, store.at[i]) for i, (src, dst) in enumerate(zip(state, new_state, strict=True))]
+    for copy in copies:
+        copy.start()
+    for copy in copies:
+        copy.wait()
     for k in range(SLICES):
-        for copy in copies[k]:
-            copy.wait()
-        for layer in range(CORES):
-            if k < down:
-                for i in range(KEPT):
-                    one, two = moments(mb[k][layer, i], vb[k][layer, i], wide(gb[k][layer, i]) * factor)
-                    mb[k][layer, i] = one
-                    vb[k][layer, i] = two
-            else:
-                rows, columns = gb[k].shape[-2:]
-                for q in range(COLORS):
-                    g = wide(gb[k][layer, q]) * factor
-                    for i, where in enumerate(lanes_of(CORES, rows, q, columns, layer)):
-                        one, two = moments(mb[k][where, :], vb[k][where, :], g[:, i * 128 : (i + 1) * 128])
-                        mb[k][where, :] = one
-                        vb[k][where, :] = two
-        pltpu.make_async_copy(mb[k], new_m[k], store.at[k, 0]).start()
-        pltpu.make_async_copy(vb[k], new_v[k], store.at[k, 1]).start()
-    for k in range(SLICES):
-        pltpu.make_async_copy(mb[k], new_m[k], store.at[k, 0]).wait()
-        pltpu.make_async_copy(vb[k], new_v[k], store.at[k, 1]).wait()
         for layer in range(CORES):
 
             def wrote(i, k=k, layer=layer):
@@ -465,6 +537,7 @@
                 *(DMA((SLICES, COLORS, side - 1)) for _ in range(4)),
                 *(DMA((SLICES,)) for _ in range(3)),
                 *(DMA((n - 1,)) for _ in range(2)),
+                *(DMA((COLORS, side)) for _ in range(4)),
             ],
             compiler_params=pltpu.CompilerParams(collective_id=0, has_side_effects=True, vmem_limit_bytes=ALL_VMEM),
         )(*views)
@@ -486,15 +559,13 @@
         gathered = pl.pallas_call(
             functools.partial(gather_kernel, side, count),
             name="gather",
-            out_shape=tuple(pltpu.VMEM((layers, COLORS, side, side, *p), bf16) for p in pieces),
+            out_shape=(*(pltpu.VMEM((layers, COLORS, side, side, *p), bf16) for p in pieces), *state, *state),
             in_specs=[VMEM] + [ANY] * 12,
-            out_specs=(VMEM,) * 3,
+            out_specs=(VMEM,) * 9,
             scratch_shapes=[
                 *(pltpu.VMEM(k.shape, bf16) for k in kept),
                 *(pltpu.VMEM((layers, KEPT, high, wide_columns), bf16) for _ in range(2)),
                 pltpu.VMEM((layers, tall, columns), bf16),
-                *state,
-                *state,
                 pltpu.VMEM((CORES + 1, *half), bf16),
                 pltpu.VMEM(pieces[2], f32),
                 *(pltpu.VMEM((KEPT, *p), bf16) for p in pieces[:2]),
@@ -502,27 +573,21 @@
                 *(DMA((SLICES, KEPT)) for _ in range(2)),
                 *(DMA((SLICES, COLORS, side - 1)) for _ in range(4)),
                 *(DMA((SLICES, COLORS, side)) for _ in range(2)),
+                *(DMA((COLORS, side)) for _ in range(4)),
             ],
-            compiler_params=pltpu.CompilerParams(collective_id=1, has_side_effects=True, vmem_limit_bytes=20 << 20),
+            compiler_params=pltpu.CompilerParams(collective_id=1, has_side_effects=True, vmem_limit_bytes=8 << 20),
         )(total, *sums, *own, *ms, *vs)
 
         gathered = [pltpu.with_memory_space_constraint(a, pltpu.VMEM) for a in gathered]
         outs = pl.pallas_call(
-            functools.partial(finish_kernel, side, count),
+            functools.partial(finish_kernel, side),
             name="finish",
             out_shape=tuple(shape(a.shape, a.dtype) for a in (*[shape(t.shape, bf16) for t in views], *ms, *vs)),
-            in_specs=[VMEM] * 4 + [ANY] * 9,
+            in_specs=[VMEM] * 9,
             out_specs=(ANY,) * 9,
-            scratch_shapes=[
-                *(pltpu.VMEM(k.shape, bf16) for k in kept),
-                *state,
-                *state,
-                DMA((SLICES, CORES, COLORS, side)),
-                DMA((SLICES, 3)),
-                DMA((SLICES, 2)),
-            ],
-            compiler_params=pltpu.CompilerParams(vmem_limit_bytes=20 << 20),
-        )(*gathered, total, *sums, *ms, *vs)
+            scratch_shapes=[DMA((SLICES, CORES, COLORS, side)), DMA((2 * SLICES,))],
+            compiler_params=pltpu.CompilerParams(vmem_limit_bytes=1 << 20),
+        )(*gathered)
         new = [a.reshape(w.shape) for a, w in zip(outs[:3], weights, strict=True)]
         rest = [
             (by_rows(a, like) if i == SLICES - 1 else a.reshape(like.shape))

time: 254 us -> 282 us (1.11)
  local copies, waits for them, and re-layouts: 0 us -> 36.1 us
  Pallas kernels: 253 us -> 245 us
    unnamed x0 -> x26, local copies, waits for them, and re-layouts: none -> 36.1 us
    pallas_call x1, Pallas kernels: 113 us -> 108 us  [step(): pl.pallas_call(functools.partial(gather_kernel, side, count), name='gathe...]
where the time goes in v2:
time: 282 us
  Pallas kernels  245 us (87%)
  local copies, waits for them, and re-layouts  36.1 us (13%)
    pallas_call x1, Pallas kernels, step(): pl.pallas_call(functools.partial(scatter_kernel, side, n), name='scatter'...  120 us
    pallas_call x1, Pallas kernels, step(): pl.pallas_call(functools.partial(gather_kernel, side, count), name='gathe...  108 us
    unnamed x26, local copies, waits for them, and re-layouts  36.1 us
    pallas_call x1, Pallas kernels, step(): pl.pallas_call(functools.partial(finish_kernel, side), name='finish', out...  16.2 us

profile of v2, /device:TPU:97, one launch (start us, length us, event | category | flops | bytes accessed | tf_op | source)
XLA Modules:
  0.0 281.9 jit_solution(12338793233374064091)
XLA Ops:
  0.6 120.4 %scatter.1 = (bf16[2,2,16,3200]{3,2,1,0:T(8,128)(2,1)}, bf16[2,2,16,3200]{3,2,1,0:T(8,128)(2,1)}, bf16[2,4,100,256]{3,2,1,0:T(8,128)(2,1)}, f32[8,128]{1,0:T(8,128)}) custom-call(bf16[2,4,4,4,16,3200]{5,4,3,2,1,0:T(8,128)(2,1)} %bitcast.48, bf16[2,4,4,4,16,3200]{5,4,3,2,1,0:T(8,128)(2,1)} %bitcast.49, bf16[2,4,4,200,1024]{4,3,2,1,0:T(8,128)(2,1)} %bitcast.50), custom_call_target="tpu_custom_call" | custom-call | tf_op jit(solution)/shard_map/scatter/pallas_call | solution.py:521
  121.1 0.0 copy-start.6
  121.1 1.1 copy-done.6
  122.2 0.0 copy-start.7
  122.2 1.1 copy-done.7
  123.4 0.0 copy-start.8
  123.4 1.1 copy-done.8
  124.5 0.0 copy-start.9
  124.5 1.0 copy-done.9
  125.5 0.0 copy-start.10
  125.5 1.0 copy-done.10
  126.5 0.0 copy-start.11
  126.5 1.0 copy-done.11
  127.5 0.0 copy-start.12
  127.5 0.7 copy-done.12
  128.2 108.3 %gather.1 = (bf16[2,4,4,4,16,3200]{5,4,3,2,1,0:T(8,128)(2,1)S(1)}, bf16[2,4,4,4,16,3200]{5,4,3,2,1,0:T(8,128)(2,1)S(1)}, bf16[2,4,4,4,200,256]{5,4,3,2,1,0:T(8,1...) custom-call(f32[8,128]{1,0:T(8,128)S(1)} %copy-done.12, ...), custom_call_target="tpu_custom_call" | custom-call | tf_op jit(solution)/shard_map/gather/pallas_call | solution.py:559
  236.5 0.0 copy-start
  236.5 4.9 %copy-done = bf16[2,4,4,4,16,3200]{5,4,3,2,1,0:T(8,128)(2,1)} copy-done((bf16[2,4,4,4,16,3200]{5,4,3,2,1,0:T(8,128)(2,1)}, bf16[2,4,4,4,16,3200]{5,4,3,2,1,0:T(8,128)(2,1)S(1)}, u32[]{:S(2)}) %copy-start) | copy-done | bytes 13107224
  241.5 0.0 copy-start.2
  241.5 4.9 %copy-done.2 = bf16[2,4,4,4,16,3200]{5,4,3,2,1,0:T(8,128)(2,1)} copy-done((bf16[2,4,4,4,16,3200]{5,4,3,2,1,0:T(8,128)(2,1)}, bf16[2,4,4,4,16,3200]{5,4,3,2,1,0:T(8,128)(2,1)S(1)}, u32[]{:S(2)}) %copy-start.2) | copy-done | bytes 13107224
  246.4 0.0 copy-start.4
  246.4 4.9 %copy-done.4 = bf16[2,4,4,4,200,256]{5,4,3,2,1,0:T(8,128)(2,1)} copy-done((bf16[2,4,4,4,200,256]{5,4,3,2,1,0:T(8,128)(2,1)}, bf16[2,4,4,4,200,256]{5,4,3,2,1,0:T(8,128)(2,1)S(1)}, u32[]{:S(2)}) %copy-start.4) | copy-done | bytes 13107224
  251.4 0.0 copy-start.1
  251.4 4.7 %copy-done.1 = bf16[2,4,4,4,16,3200]{5,4,3,2,1,0:T(8,128)(2,1)S(1)} copy-done((bf16[2,4,4,4,16,3200]{5,4,3,2,1,0:T(8,128)(2,1)S(1)}, bf16[2,4,4,4,16,3200]{5,4,3,2,1,0:T(8,128)(2,1)}, u32[]{:S(2)}) %copy-start.1) | copy-done | bytes 13107224
  256.1 0.0 copy-start.3
  256.1 4.7 %copy-done.3 = bf16[2,4,4,4,16,3200]{5,4,3,2,1,0:T(8,128)(2,1)S(1)} copy-done((bf16[2,4,4,4,16,3200]{5,4,3,2,1,0:T(8,128)(2,1)S(1)}, bf16[2,4,4,4,16,3200]{5,4,3,2,1,0:T(8,128)(2,1)}, u32[]{:S(2)}) %copy-start.3) | copy-done | bytes 13107224
  260.8 0.0 copy-start.5
  260.8 4.7 %copy-done.5 = bf16[2,4,4,4,200,256]{5,4,3,2,1,0:T(8,128)(2,1)S(1)} copy-done((bf16[2,4,4,4,200,256]{5,4,3,2,1,0:T(8,128)(2,1)S(1)}, bf16[2,4,4,4,200,256]{5,4,3,2,1,0:T(8,128)(2,1)}, u32[]{:S(2)}) %copy-start.5) | copy-done | bytes 13107224
  265.5 16.2 %finish.1 = (bf16[2,4,4,4,16,3200]{5,4,3,2,1,0:T(8,128)(2,1)}, bf16[2,4,4,4,16,3200]{5,4,3,2,1,0:T(8,128)(2,1)}, bf16[2,4,4,200,1024]{4,3,2,1,0:T(8,128)(2,1)}, ...) custom-call(bf16[2,4,4,4,16,3200]{5,4,3,2,1,0:T(8,128)(2,1)S(1)} %co, ...), custom_call_target="tpu_custom_call" | custom-call | tf_op jit(solution)/shard_map/finish/pallas_call | solution.py:582
Async XLA Ops:
  121.1 1.1 copy-start.6
  122.2 1.1 copy-start.7
  123.4 1.1 copy-start.8
  124.5 1.0 copy-start.9
  125.5 1.0 copy-start.10
  126.5 1.0 copy-start.11
  127.5 0.7 copy-start.12
  236.5 5.0 %copy-start = (bf16[2,4,4,4,16,3200]{5,4,3,2,1,0:T(8,128)(2,1)}, bf16[2,4,4,4,16,3200]{5,4,3,2,1,0:T(8,128)(2,1)S(1)}, u32[]{:S(2)}) copy-start(bf16[2,4,4,4,16,3200]{5,4,3,2,1,0:T(8,128)(2,1)S(1)} %get-tuple-element.35.refs_0_) | copy-start | bytes 39321604
  241.5 4.9 %copy-start.2 = (bf16[2,4,4,4,16,3200]{5,4,3,2,1,0:T(8,128)(2,1)}, bf16[2,4,4,4,16,3200]{5,4,3,2,1,0:T(8,128)(2,1)S(1)}, u32[]{:S(2)}) copy-start(bf16[2,4,4,4,16,3200]{5,4,3,2,1,0:T(8,128)(2,1)S(1)} %get-tuple-element.36.refs_1_) | copy-start | bytes 39321604
  246.4 4.9 %copy-start.4 = (bf16[2,4,4,4,200,256]{5,4,3,2,1,0:T(8,128)(2,1)}, bf16[2,4,4,4,200,256]{5,4,3,2,1,0:T(8,128)(2,1)S(1)}, u32[]{:S(2)}) copy-start(bf16[2,4,4,4,200,256]{5,4,3,2,1,0:T(8,128)(2,1)S(1)} %get-tuple-element.37.refs_2_) | copy-start | bytes 39321604
  251.4 4.7 %copy-start.1 = (bf16[2,4,4,4,16,3200]{5,4,3,2,1,0:T(8,128)(2,1)S(1)}, bf16[2,4,4,4,16,3200]{5,4,3,2,1,0:T(8,128)(2,1)}, u32[]{:S(2)}) copy-start(bf16[2,4,4,4,16,3200]{5,4,3,2,1,0:T(8,128)(2,1)} %copy-done) | copy-start | bytes 39321604
  256.1 4.7 %copy-start.3 = (bf16[2,4,4,4,16,3200]{5,4,3,2,1,0:T(8,128)(2,1)S(1)}, bf16[2,4,4,4,16,3200]{5,4,3,2,1,0:T(8,128)(2,1)}, u32[]{:S(2)}) copy-start(bf16[2,4,4,4,16,3200]{5,4,3,2,1,0:T(8,128)(2,1)} %copy-done.2) | copy-start | bytes 39321604
  260.8 4.7 %copy-start.5 = (bf16[2,4,4,4,200,256]{5,4,3,2,1,0:T(8,128)(2,1)S(1)}, bf16[2,4,4,4,200,256]{5,4,3,2,1,0:T(8,128)(2,1)}, u32[]{:S(2)}) copy-start(bf16[2,4,4,4,200,256]{5,4,3,2,1,0:T(8,128)(2,1)} %copy-done.4) | copy-start | bytes 39321604

commit v3 on v2

--- a/solution.py
+++ b/solution.py
@@ -575,7 +575,7 @@
                 *(DMA((SLICES, COLORS, side)) for _ in range(2)),
                 *(DMA((COLORS, side)) for _ in range(4)),
             ],
-            compiler_params=pltpu.CompilerParams(collective_id=1, has_side_effects=True, vmem_limit_bytes=8 << 20),
+            compiler_params=pltpu.CompilerParams(collective_id=1, has_side_effects=True, vmem_limit_bytes=20 << 20),
         )(total, *sums, *own, *ms, *vs)
 
         gathered = [pltpu.with_memory_space_constraint(a, pltpu.VMEM) for a in gathered]
@@ -586,7 +586,7 @@
             in_specs=[VMEM] * 9,
             out_specs=(ANY,) * 9,
             scratch_shapes=[DMA((SLICES, CORES, COLORS, side)), DMA((2 * SLICES,))],
-            compiler_params=pltpu.CompilerParams(vmem_limit_bytes=1 << 20),
+            compiler_params=pltpu.CompilerParams(vmem_limit_bytes=20 << 20),
         )(*gathered)
         new = [a.reshape(w.shape) for a, w in zip(outs[:3], weights, strict=True)]
         rest = [

time: 282 us -> 247 us (0.88)
  local copies, waits for them, and re-layouts: 36.1 us -> 0 us
    unnamed x26 -> x0, local copies, waits for them, and re-layouts: 36.1 us -> none
where the time goes in v3:
time: 247 us; the launch traced here: 246 us
  Pallas kernels  246 us (100%)
    pallas_call x1, Pallas kernels, step(): pl.pallas_call(functools.partial(scatter_kernel, side, n), name='scatter'...  120 us
    pallas_call x1, Pallas kernels, step(): pl.pallas_call(functools.partial(gather_kernel, side, count), name='gathe...  109 us
    pallas_call x1, Pallas kernels, step(): pl.pallas_call(functools.partial(finish_kernel, side), name='finish', out...  16.2 us

profile of v3, /device:TPU:97, one launch (start us, length us, event | category | flops | bytes accessed | tf_op | source)
XLA Modules:
  0.0 246.5 jit_solution(10386042630474323734)
XLA Ops:
  0.6 120.4 %scatter.1 = (bf16[2,2,16,3200]{3,2,1,0:T(8,128)(2,1)}, bf16[2,2,16,3200]{3,2,1,0:T(8,128)(2,1)}, bf16[2,4,100,256]{3,2,1,0:T(8,128)(2,1)}, f32[8,128]{1,0:T(8,128)}) custom-call(bf16[2,4,4,4,16,3200]{5,4,3,2,1,0:T(8,128)(2,1)} %bitcast.45, bf16[2,4,4,4,16,3200]{5,4,3,2,1,0:T(8,128)(2,1)} %bitcast.46, bf16[2,4,4,200,1024]{4,3,2,1,0:T(8,128)(2,1)} %bitcast.47), custom_call_target="tpu_custom_call" | custom-call | tf_op jit(solution)/shard_map/scatter/pallas_call | solution.py:521
  121.1 109.0 %gather.1 = (bf16[2,4,4,4,16,3200]{5,4,3,2,1,0:T(8,128)(2,1)S(1)}, bf16[2,4,4,4,16,3200]{5,4,3,2,1,0:T(8,128)(2,1)S(1)}, bf16[2,4,4,4,200,256]{5,4,3,2,1,0:T(8,1...) custom-call(f32[8,128]{1,0:T(8,128)} %get-tuple-element.31.refs_0_, ...), custom_call_target="tpu_custom_call" | custom-call | tf_op jit(solution)/shard_map/gather/pallas_call | solution.py:559
  230.1 16.2 %finish.1 = (bf16[2,4,4,4,16,3200]{5,4,3,2,1,0:T(8,128)(2,1)}, bf16[2,4,4,4,16,3200]{5,4,3,2,1,0:T(8,128)(2,1)}, bf16[2,4,4,200,1024]{4,3,2,1,0:T(8,128)(2,1)}, ...) custom-call(bf16[2,4,4,4,16,3200]{5,4,3,2,1,0:T(8,128)(2,1)S(1)} %ge, ...), custom_call_target="tpu_custom_call" | custom-call | tf_op jit(solution)/shard_map/finish/pallas_call | solution.py:582

commit v4 on v0

v4 whole, which is shorter than its diff:
```python
import functools
import math

import jax
import jax.numpy as jnp
from jax import lax
from jax.experimental import pallas as pl
from jax.experimental.pallas import tpu as pltpu
from jax.sharding import PartitionSpec as P

MESH = pl.DeviceIdType.MESH
CORES = 2
COLORS = 4
SLICES = 3
KEPT = COLORS // CORES
ANY = pl.BlockSpec(memory_space=pl.ANY)
VMEM = pl.BlockSpec(memory_space=pltpu.VMEM)
DMA = pltpu.SemaphoreType.DMA


def each(n, body):
    lax.fori_loop(0, n, lambda i, _: body(i), None)


class Place:
    def __init__(self, side):
        self.side = side
        self.me = lax.axis_index("dp")
        self.core = lax.rem(self.me, CORES)
        self.chip = self.me // CORES
        self.x, self.y = self.chip // side, lax.rem(self.chip, side)
        self.partner = self.me + 1 - 2 * self.core

    def at(self, x, y):
        return (x * self.side + y) * CORES + self.core

    def moved(self, p, by):
        return lax.rem(p + by + 2 * self.side, self.side)

    def way(self, q):
        on_x = q < COLORS // 2
        return jnp.where(on_x, self.x, self.y), jnp.where(on_x, self.y, self.x), 1 - 2 * lax.rem(q, 2)

    def next(self, q, first):
        up = 1 - 2 * lax.rem(q, 2)
        on_x = (q < COLORS // 2) == first
        return self.at(jnp.where(on_x, self.moved(self.x, up), self.x), jnp.where(on_x, self.y, self.moved(self.y, up)))


def remote(src, dst, send, recv, device):
    return pltpu.make_async_remote_copy(
        src_ref=src, dst_ref=dst, send_sem=send, recv_sem=recv, device_id={"dp": device}, device_id_type=MESH
    )


def meet(at):
    barrier = pltpu.get_barrier_semaphore()
    near = [at.partner] + [at.next(q, True) for q in range(COLORS)]
    for device in near:
        pl.semaphore_signal(barrier, inc=1, device_id={"dp": device}, device_id_type=MESH)
    return lambda: pl.semaphore_wait(barrier, len(near))


def part(ref, k, layer, q, t, columns):
    if k < SLICES - 1:
        return ref.at[layer, t, :, q] if q < COLORS // 2 else ref.at[layer, :, t, q]
    c = pl.ds(q * columns, columns)
    return ref.at[layer, t, :, :, c] if q < COLORS // 2 else ref.at[layer, :, t, :, c]


def wide(x):
    return x.astype(jnp.float32)


def squares(g):
    total = jnp.zeros((8, 128), jnp.float32)
    for r in range(0, g.shape[0], 8):
        for c in range(0, g.shape[1], 128):
            block = g[r : r + 8, c : c + 128]
            total += block * block
    return total


def factor_of(total, count):
    return jnp.minimum(1.0, 0.5 * lax.rsqrt(jnp.sum(total) / count + 1e-30))


def moments(m, v, g):
    return 0.9 * m + 0.1 * g, 0.95 * v + 0.05 * g * g


def new_weight(w, m, v, g):
    m, v = moments(m, v, g)
    return (w - 0.02 * (m * lax.rsqrt(v + 1e-8) + 0.1 * w)).astype(jnp.bfloat16)


def lanes_of(layers, rows, q, columns, layer):
    per_row = COLORS * columns // 128 * layers
    return [pl.ds((q * columns // 128 + i) * layers + layer, rows, stride=per_row) for i in range(columns // 128)]


def step_kernel(side, n, count, *refs):
    terms, weights, m, v = refs[0:3], refs[3:6], refs[6:9], refs[9:12]
    out, mb, vb = refs[12:15], refs[15:18], refs[18:21]
    r1, r2, fin, lent_sums = refs[21:24], refs[24:27], refs[27:30], refs[30:33]
    half_w, tmp, norms = refs[33:36]
    load, push_s, push_r, state_in = refs[36:40]
    s1, v1, s2, v2 = refs[40:44]
    piece_s, piece_r, s1_piece, v1_piece = refs[44:48]
    norm_s, norm_r, sum_s, sum_r = refs[48:52]
    rows_in, swap_s, swap_r = refs[52:55]
    t1, u1, t2, u2 = refs[55:59]
    give_s, give_r, t2_piece, u2_piece, give_piece_s, give_piece_r = refs[59:65]
    at = Place(side)
    me, core, partner = at.me, at.core, at.partner
    other = 1 - core
    last = side - 1
    down = SLICES - 1
    rows, columns = half_w.shape[-2:]

    def group(q, s):
        p1, _, up = at.way(q)
        return at.moved(p1, -up * (1 + s))

    def loads(k, s):
        for q in range(COLORS):
            t = group(q, s)
            pltpu.make_async_copy(part(terms[k], k, core, q, t, columns), out[k].at[core, q, t], load.at[k, q, s]).start()

    def pushed(k, q, s, src=None):
        dst = out[k].at[core, q, group(q, s)]
        return remote(dst if src is None else src, dst, push_s.at[k, q, s], push_r.at[k, q, s], partner)

    def pushes(k, s):
        for q in range(COLORS):
            pushed(k, q, s, part(terms[k], k, other, q, group(q, s), columns)).start()

    def loaded(k, q, s):
        ref = out[k].at[core, q, group(q, s)]
        pltpu.make_async_copy(ref, ref, load.at[k, q, s]).wait()

    def ready(k, q, s):
        loaded(k, q, s)
        pushed(k, q, s).wait_recv()

    def pushed_piece(q, j, src=None):
        dst = out[0].at[core, q, group(q, 0), j]
        return remote(dst if src is None else src, dst, piece_s.at[q, j], piece_r.at[q, j], partner)

    def sum1_piece(q, j):
        src = out[0].at[core, q, group(q, 0), j]
        return remote(src, r1[0].at[q, 0, j], s1_piece.at[q, j], v1_piece.at[q, j], at.next(q, True))

    def sum1(k, q, s):
        src = r1[k].at[q, s - 1] if s else out[k].at[core, q, group(q, s)]
        return remote(src, r1[k].at[q, s], s1.at[k, q, s], v1.at[k, q, s], at.next(q, True))

    def sum2(k, q, s):
        _, p2, up = at.way(q)
        src = r2[k].at[q, s - 1] if s else r1[k].at[q, last - 1, at.moved(p2, -up)]
        return remote(src, r2[k].at[q, s], s2.at[k, q, s], v2.at[k, q, s], at.next(q, False))

    greet = meet(at)
    for k in range(SLICES):
        loads(k, 0)
    greet()
    for j in range(side):
        for q in range(COLORS):
            pushed_piece(q, j, part(terms[0], 0, other, q, group(q, 0), columns).at[j]).start()
    for k in range(1, SLICES):
        pushes(k, 0)

    def both(k, q, t, j):
        return wide(out[k][0, q, t, j]) + wide(out[k][1, q, t, j])

    for j in range(side):

        def start(q):
            t = group(q, 0)
            if j == 0:
                loaded(0, q, 0)
            pushed_piece(q, j).wait_recv()
            out[0][core, q, t, j] = both(0, q, t, j).astype(jnp.bfloat16)
            sum1_piece(q, j).start()

        each(COLORS, start)
    loads(0, 1)
    pushes(0, 1)
    for s in range(last):
        for k in range(SLICES):
            if s == 0 and k == 0:
                continue

            def first(q):
                t = group(q, s)
                if s == 1 and k == 0:
                    each(side, lambda j: sum1_piece(q, j).wait_recv())
                elif s:
                    sum1(k, q, s - 1).wait_recv()
                ready(k, q, s)

                def add(j):
                    if s:
                        r1[k][q, s - 1, j] = (wide(r1[k][q, s - 1, j]) + both(k, q, t, j)).astype(jnp.bfloat16)
                    else:
                        out[k][core, q, t, j] = both(k, q, t, j).astype(jnp.bfloat16)

                each(side, add)
                sum1(k, q, s).start()

            each(COLORS, first)
            loads(k, s + 1)
            pushes(k, s + 1)
        if s == 0:
            moments_in = [
                pltpu.make_async_copy(src[k], dst[k], state_in.at[k, i])
                for k in range(SLICES)
                for i, (src, dst) in enumerate(((m, mb), (v, vb)))
            ]
            for copy in moments_in:
                copy.start()

    def here(k, q, u):
        p1, _, _ = at.way(q)
        return both(k, q, p1, u) + wide(r1[k][q, last - 1, u])

    for s in range(last):
        for k in range(SLICES):

            def second(q):
                _, p2, up = at.way(q)
                u = at.moved(p2, -up * (1 + s))
                if s:
                    sum2(k, q, s - 1).wait_recv()
                    r2[k][q, s - 1] = (wide(r2[k][q, s - 1]) + here(k, q, u)).astype(jnp.bfloat16)
                else:
                    sum1(k, q, last - 1).wait_recv()
                    ready(k, q, last)
                    r1[k][q, last - 1, u] = here(k, q, u).astype(jnp.bfloat16)
                sum2(k, q, s).start()

            each(COLORS, second)

    def share(k, of):
        return fin[k].at[pl.ds(of * KEPT, KEPT)] if k < down else fin[k].at[of]

    def swap_sums(k):
        return remote(share(k, other), lent_sums[k], sum_s.at[k], sum_r.at[k], partner)

    def norm(i):
        return remote(norms.at[me], norms.at[me], norm_s.at[i], norm_r.at[i], lax.rem(me + 1 + i, n))

    norms[me] = jnp.zeros((8, 128), jnp.float32)
    for k in range(SLICES):

        def end(q):
            _, p2, _ = at.way(q)
            sum2(k, q, last - 1).wait_recv()
            g = (wide(r2[k][q, last - 1]) + here(k, q, p2)).astype(jnp.bfloat16)
            norms[me] += squares(wide(g))
            if k < down:
                fin[k][q] = g
            else:
                tmp[...] = wide(g)
                for h in range(CORES):
                    fin[k][h, q] = tmp[h * rows : (h + 1) * rows].astype(jnp.bfloat16)

            if k:
                sum1(k, q, 0).wait_send()
            else:
                each(side, lambda j: sum1_piece(q, j).wait_send())

        each(COLORS, end)
        if k < down:
            swap_sums(k).start()
    each(n - 1, lambda i: norm(i).start())
    swap_sums(down).start()
    for k in range(SLICES):

        def drain(q):
            for s in range(side):
                if k or s:
                    pushed(k, q, s).wait_send()
            for s in range(last):
                if s:
                    sum1(k, q, s).wait_send()
                sum2(k, q, s).wait_send()
            if k == 0:
                each(side, lambda j: pushed_piece(q, j).wait_send())

        each(COLORS, drain)

    def old(k, layer, i):
        return r1[k].at[0, 0, layer * KEPT + i] if k < down else r1[k].at[layer, 0, i]

    def rows_of(k):
        for layer in range(CORES):
            for i in range(KEPT if k < down else COLORS):
                if k < down:
                    src = weights[k].at[layer, me, i]
                else:
                    src = weights[k].at[layer, at.chip, :, pl.ds(i * columns, columns)]
                yield pltpu.make_async_copy(src, old(k, layer, i), rows_in.at[k, layer, i])

    for k in range(SLICES):
        for copy in rows_of(k):
            copy.start()
    for copy in moments_in:
        copy.wait()
    for k in range(SLICES):
        swap_sums(k).wait_recv()
        for copy in rows_of(k):
            copy.wait()
    each(n - 1, lambda i: norm(i).wait_recv())
    tmp[0:8, 0:128] = jnp.zeros((8, 128), jnp.float32)

    def tally(i):
        tmp[0:8, 0:128] += norms[i]

    each(n, tally)
    factor = factor_of(tmp[0:8, 0:128], count)

    def swap(k, i, q, layer):
        p1, p2, _ = at.way(q)
        return remote(r2[k].at[i, 0], out[k].at[layer, q, p1, p2], swap_s.at[k, i], swap_r.at[k, i], partner)

    def hop1(k, q, s):
        p1, p2, up = at.way(q)
        ref = out[k].at[core, q, p1, at.moved(p2, -up * s)]
        return remote(ref, ref, t1.at[k, q, s], u1.at[k, q, s], at.next(q, False))

    def hop2(k, q, s):
        p1, _, up = at.way(q)
        ref = out[k].at[core, q, at.moved(p1, -up * s)]
        return remote(ref, ref, t2.at[k, q, s], u2.at[k, q, s], at.next(q, True))

    def give(k, q, s, layer):
        p1, _, up = at.way(q)
        ref = out[k].at[layer, q, at.moved(p1, -up * s)]
        return remote(ref, ref, give_s.at[k, q, s], give_r.at[k, q, s], partner)

    def hop2_piece(q, j):
        p1, _, up = at.way(q)
        ref = out[down].at[core, q, at.moved(p1, -up * (last - 1)), j]
        return remote(ref, ref, t2_piece.at[q, j], u2_piece.at[q, j], at.next(q, True))

    def give_piece(q, j, layer):
        p1, _, up = at.way(q)
        ref = out[down].at[layer, q, at.moved(p1, -up * last), j]
        return remote(ref, ref, give_piece_s.at[q, j], give_piece_r.at[q, j], partner)

    def gradient(k, mine, i):
        if k < down:
            return wide(fin[k][core * KEPT + i] if mine else lent_sums[k][i]) * factor
        return wide(fin[k][core, i] if mine else lent_sums[k][i]) * factor

    def step(k):
        for layer, mine in ((core, True), (other, False)):
            for i in range(KEPT):
                q = core * KEPT + i
                w = new_weight(wide(old(k, layer, i)[...]), mb[k][layer, i], vb[k][layer, i], gradient(k, mine, i))
                if mine:
                    p1, p2, _ = at.way(q)
                    out[k][layer, q, p1, p2] = w
                    hop1(k, q, 0).start()
                else:
                    r2[k][i, 0] = w
                    swap(k, i, q, other).start()

    def swapped(k):
        for i in range(KEPT):
            q = other * KEPT + i
            swap(k, i, q, core).wait_recv()
            hop1(k, q, 0).start()

    half_swap = remote(fin[down].at[other], half_w.at[1], swap_s.at[down, 0], swap_r.at[down, 0], partner)

    def for_layer(mine, body):
        for layer in range(CORES):
            pl.when((layer == core) == mine)(functools.partial(body, layer))

    def step_down(mine):
        def body(layer):
            for q in range(COLORS):
                tmp[...] = wide(old(down, layer, q)[...])
                w = jnp.where(core == 0, tmp[0:rows], tmp[rows : 2 * rows])
                where = lanes_of(CORES, rows, q, columns, layer)
                one = jnp.concatenate([mb[down][i, :] for i in where], axis=1)
                two = jnp.concatenate([vb[down][i, :] for i in where], axis=1)
                w = new_weight(w, one, two, gradient(down, mine, q))
                if mine:
                    half_w[0, q] = w
                else:
                    fin[down][other, q] = w

        for_layer(mine, body)

    def keep_moments(k):
        for mine in (True, False):
            if k < down:
                layer = core if mine else other
                for i in range(KEPT):
                    one, two = moments(mb[k][layer, i], vb[k][layer, i], gradient(k, mine, i))
                    mb[k][layer, i] = one
                    vb[k][layer, i] = two
                continue

            def body(layer, mine=mine):
                for q in range(COLORS):
                    g = gradient(down, mine, q)
                    for i, where in enumerate(lanes_of(CORES, rows, q, columns, layer)):
                        one, two = moments(mb[k][where, :], vb[k][where, :], g[:, i * 128 : (i + 1) * 128])
                        mb[k][where, :] = one
                        vb[k][where, :] = two

            for_layer(mine, body)

    step(0)
    step(1)
    swapped(0)
    swap_sums(down).wait_send()
    step_down(False)
    half_swap.start()
    swapped(1)
    step_down(True)
    half_swap.wait_recv()
    for q in range(COLORS):
        p1, p2, _ = at.way(q)
        tmp[0:rows] = wide(half_w[core, q])
        tmp[rows : 2 * rows] = wide(half_w[other, q])
        out[down][core, q, p1, p2] = tmp[...].astype(jnp.bfloat16)
        hop1(down, q, 0).start()

    for s in range(1, last):
        for k in range(SLICES):

            def spread(q):
                hop1(k, q, s - 1).wait_recv()
                hop1(k, q, s).start()

            each(COLORS, spread)
    for s in range(side):
        for k in range(SLICES):

            def onward(q):
                if s:
                    hop2(k, q, s - 1).wait_recv()
                else:
                    hop1(k, q, last - 1).wait_recv()
                if k == down and s == last - 1:
                    each(side, lambda j: hop2_piece(q, j).start())
                elif s < last:
                    hop2(k, q, s).start()
                give(k, q, s, core).start()

            def onward_piece(i):
                j, q = i // COLORS, lax.rem(i, COLORS)
                hop2_piece(q, j).wait_recv()
                give_piece(q, j, core).start()

            if k == down and s == last:
                each(side * COLORS, onward_piece)
            else:
                each(COLORS, onward)
            if s == 0:
                keep_moments(k)

    for k in range(SLICES):

        def settle(q):
            cut = 1 if k == down else 0
            for s in range(side - cut):
                give(k, q, s, other).wait_recv()
                give(k, q, s, core).wait_send()
            for s in range(last):
                hop1(k, q, s).wait_send()
                if s < last - cut:
                    hop2(k, q, s).wait_send()
            if cut:

                def pieces(j):
                    give_piece(q, j, other).wait_recv()
                    give_piece(q, j, core).wait_send()
                    hop2_piece(q, j).wait_send()

                each(side, pieces)

        each(COLORS, settle)
        if k < down:
            swap_sums(k).wait_send()
            for i in range(KEPT):
                swap(k, i, core * KEPT + i, other).wait_send()
    half_swap.wait_send()
    each(n - 1, lambda i: norm(i).wait_send())


def finish_kernel(side, *refs):
    whole, state, new, new_state, write, store = refs[0:3], refs[3:9], refs[9:12], refs[12:18], refs[18], refs[19]
    for k in range(SLICES):
        for layer in range(CORES):
            for q in range(COLORS):

                def put(t, k=k, layer=layer, q=q):
                    src, dst = whole[k].at[layer, q, t], part(new[k], k, layer, q, t, whole[k].shape[-1])
                    pltpu.make_async_copy(src, dst, write.at[k, layer, q, t]).start()

                each(side, put)
    copies = [pltpu.make_async_copy(src, dst, store.at[i]) for i, (src, dst) in enumerate(zip(state, new_state, strict=True))]
    for copy in copies:
        copy.start()
    for copy in copies:
        copy.wait()
    for k in range(SLICES):
        for layer in range(CORES):

            def wrote(i, k=k, layer=layer):
                q, t = i // side, lax.rem(i, side)
                pltpu.make_async_copy(whole[k].at[layer, q, t], whole[k].at[layer, q, t], write.at[k, layer, q, t]).wait()

            each(COLORS * side, wrote)


def solution(mesh):
    n = mesh.shape["dp"]
    side = math.isqrt(n // CORES)
    bf16, f32 = jnp.bfloat16, jnp.float32
    shape = jax.ShapeDtypeStruct

    def step(*arrays):
        terms, weights, m, v = (arrays[i : i + 3] for i in (0, 3, 6, 9))
        layers, depth, wide_columns = weights[0].shape
        _, deep, columns = weights[2].shape
        chips = side * side
        high, tall = depth // chips // COLORS, deep // chips
        pieces = [(high, wide_columns)] * 2 + [(tall, columns // COLORS)]
        half = (COLORS, tall // CORES, columns // COLORS)
        count = sum(w.size for w in weights)

        views = [t.reshape(layers, side, side, COLORS, high, wide_columns) for t in terms[:2]]
        views.append(terms[2].reshape(layers, side, side, tall, columns))
        def by_lanes(a):
            layers, rows, columns = a.shape
            a = a.transpose(1, 0, 2).reshape(rows, layers, columns // 128, 128)
            return a.transpose(0, 2, 1, 3).reshape(-1, 128)

        def by_rows(a, like):
            layers, rows, columns = like.shape
            a = a.reshape(rows, columns // 128, layers, 128).transpose(0, 2, 1, 3)
            return a.reshape(rows, layers, columns).transpose(1, 0, 2)

        own = [w.reshape(layers, n, KEPT, high, wide_columns) for w in weights[:2]]
        own.append(weights[2].reshape(layers, chips, tall, columns))
        ms, vs = ([a.reshape(layers, KEPT, high, wide_columns) for a in b[:2]] + [by_lanes(b[2])] for b in (m, v))
        state = [pltpu.VMEM(a.shape, f32) for a in ms]
        gathered = pl.pallas_call(
            functools.partial(step_kernel, side, n, count),
            name="step",
            out_shape=(*(pltpu.VMEM((layers, COLORS, side, side, *p), bf16) for p in pieces), *state, *state),
            in_specs=[ANY] * 12,
            out_specs=(VMEM,) * 9,
            scratch_shapes=[
                *(pltpu.VMEM((COLORS, side - 1, side, *p), bf16) for p in pieces),
                *(pltpu.VMEM((COLORS, side - 1, *p), bf16) for p in pieces),
                *(pltpu.VMEM((COLORS, *p), bf16) for p in pieces[:2]),
                pltpu.VMEM((CORES, *half), bf16),
                *(pltpu.VMEM((KEPT, *p), bf16) for p in pieces[:2]),
                pltpu.VMEM(half, bf16),
                pltpu.VMEM((CORES, *half), bf16),
                pltpu.VMEM(pieces[2], f32),
                pltpu.VMEM((n, 8, 128), f32),
                *(DMA((SLICES, COLORS, side)) for _ in range(3)),
                DMA((SLICES, 2)),
                *(DMA((SLICES, COLORS, side - 1)) for _ in range(4)),
                *(DMA((COLORS, side)) for _ in range(4)),
                *(DMA((n - 1,)) for _ in range(2)),
                *(DMA((SLICES,)) for _ in range(2)),
                DMA((SLICES, CORES, COLORS)),
                *(DMA((SLICES, KEPT)) for _ in range(2)),
                *(DMA((SLICES, COLORS, side - 1)) for _ in range(4)),
                *(DMA((SLICES, COLORS, side)) for _ in range(2)),
                *(DMA((COLORS, side)) for _ in range(4)),
            ],
            compiler_params=pltpu.CompilerParams(collective_id=0, has_side_effects=True, vmem_limit_bytes=22_806_528),
        )(*views, *own, *ms, *vs)
        gathered = [pltpu.with_memory_space_constraint(a, pltpu.VMEM) for a in gathered]
        outs = pl.pallas_call(
            functools.partial(finish_kernel, side),
            name="finish",
            out_shape=tuple(shape(a.shape, a.dtype) for a in (*[shape(t.shape, bf16) for t in views], *ms, *vs)),
            in_specs=[VMEM] * 9,
            out_specs=(ANY,) * 9,
            scratch_shapes=[DMA((SLICES, CORES, COLORS, side)), DMA((2 * SLICES,))],
            compiler_params=pltpu.CompilerParams(vmem_limit_bytes=22_806_528),
        )(*gathered)
        new = [a.reshape(w.shape) for a, w in zip(outs[:3], weights, strict=True)]
        rest = [
            (by_rows(a, like) if i == SLICES - 1 else a.reshape(like.shape))
            for block in (outs[3:6], outs[6:9])
            for i, (a, like) in enumerate(zip(block, m, strict=True))
        ]
        return (*new, *rest)

    all_of, cut = P(None, None, None), P(None, "dp", None)
    return jax.shard_map(
        step,
        mesh=mesh,
        in_specs=(P(("rep", "dp"), None, None, None),) * 3 + (all_of,) * 3 + (cut,) * 6,
        out_specs=(P("rep", None, None),) * 3 + (P("rep", "dp", None),) * 6,
        check_vma=False,
    )
```

time: 621 us -> 243 us (0.39)
  waiting for transfers between devices: 483 us -> 0 us
  Pallas kernels: 0 us -> 242 us
  local copies, waits for them, and re-layouts: 57 us -> 0 us
  blocking collectives: 46.5 us -> 0 us
  other arithmetic: 17.2 us -> 0 us
  between operations: 16.9 us -> 0.82 us
    pallas_call x0 -> x2, Pallas kernels: none -> 242 us  [the longest x1 226 us: step(): pl.pallas_call(functools.partial(step_kernel, side, n, count), name='step...]
    reduce_scatter x2 -> x0, waiting for transfers between devices: 196 us -> none  [step(): lax.psum_scatter(t[0], 'dp', scatter_dimension=1, tiled=True)]
    all_gather x3 -> x0, waiting for transfers between devices: 159 us -> none  [step(): whole = [lax.all_gather(one[0], 'dp', axis=1, tiled=True) for one in new]]
    unnamed x7 -> x0, waiting for transfers between devices: 127 us -> none
    unnamed x12 -> x0, local copies, waits for them, and re-layouts: 55.9 us -> none
    psum x1 -> x0, blocking collectives: 46.5 us -> none  [step(): squares = lax.psum(sum((jnp.sum(g * g) for g in gradients)), 'dp')]
    convert_element_type x3 -> x0, other arithmetic: 11.1 us -> none  [adamw(): return ((w - 0.02 * step).astype(jnp.bfloat16), m, v)]
  transfers between devices with their start and end apart: 6 -> 0, of which waited for: 6 -> 0; matrix products, arithmetic and copies ran while one was open for 4% -> 0% of each run, Pallas kernels for 0% -> 0%
where the time goes in v4:
time: 243 us
  Pallas kernels  242 us (100%)
    pallas_call x1, Pallas kernels, step(): pl.pallas_call(functools.partial(step_kernel, side, n, count), name='step...  226 us
    pallas_call x1, Pallas kernels, step(): pl.pallas_call(functools.partial(finish_kernel, side), name='finish', out...  16.2 us

profile of v4, /device:TPU:97, one launch (start us, length us, event | category | flops | bytes accessed | tf_op | source)
XLA Modules:
  0.0 242.7 jit_solution(9326228171367647481)
XLA Ops:
  0.6 225.7 %step.1 = (bf16[2,4,4,4,16,3200]{5,4,3,2,1,0:T(8,128)(2,1)S(1)}, bf16[2,4,4,4,16,3200]{5,4,3,2,1,0:T(8,128)(2,1)S(1)}, bf16[2,4,4,4,200,256]{5,4,3,2,1,0:T(8,128...) custom-call(bf16[2,4,4,4,16,3200]{5,4,3,2,1,0:T(8,128)(2,1)} %bitcas, ...), custom_call_target="tpu_custom_call" | custom-call | tf_op jit(solution)/shard_map/step/pallas_call | solution.py:555
  226.4 16.2 %finish.1 = (bf16[2,4,4,4,16,3200]{5,4,3,2,1,0:T(8,128)(2,1)}, bf16[2,4,4,4,16,3200]{5,4,3,2,1,0:T(8,128)(2,1)}, bf16[2,4,4,200,1024]{4,3,2,1,0:T(8,128)(2,1)}, ...) custom-call(bf16[2,4,4,4,16,3200]{5,4,3,2,1,0:T(8,128)(2,1)S(1)} %ge, ...), custom_call_target="tpu_custom_call" | custom-call | tf_op jit(solution)/shard_map/finish/pallas_call | solution.py:586

commit v5 on v4

--- a/solution.py
+++ b/solution.py
@@ -261,9 +261,7 @@
             if k < down:
                 fin[k][q] = g
             else:
-                tmp[...] = wide(g)
-                for h in range(CORES):
-                    fin[k][h, q] = tmp[h * rows : (h + 1) * rows].astype(jnp.bfloat16)
+                r2[k][q, last - 1] = g
 
             if k:
                 sum1(k, q, 0).wait_send()
@@ -274,6 +272,13 @@
         if k < down:
             swap_sums(k).start()
     each(n - 1, lambda i: norm(i).start())
+
+    def halve(q):
+        tmp[...] = wide(r2[down][q, last - 1])
+        for h in range(CORES):
+            fin[down][h, q] = tmp[h * rows : (h + 1) * rows].astype(jnp.bfloat16)
+
+    each(COLORS, halve)
     swap_sums(down).start()
     for k in range(SLICES):
 
@@ -312,13 +317,7 @@
         for copy in rows_of(k):
             copy.wait()
     each(n - 1, lambda i: norm(i).wait_recv())
-    tmp[0:8, 0:128] = jnp.zeros((8, 128), jnp.float32)
-
-    def tally(i):
-        tmp[0:8, 0:128] += norms[i]
-
-    each(n, tally)
-    factor = factor_of(tmp[0:8, 0:128], count)
+    factor = factor_of(jnp.sum(norms[...], axis=0), count)
 
     def swap(k, i, q, layer):
         p1, p2, _ = at.way(q)
@@ -496,28 +495,23 @@
 
 def finish_kernel(side, *refs):
     whole, state, new, new_state, write, store = refs[0:3], refs[3:9], refs[9:12], refs[12:18], refs[18], refs[19]
+    copies = []
     for k in range(SLICES):
         for layer in range(CORES):
             for q in range(COLORS):
-
-                def put(t, k=k, layer=layer, q=q):
-                    src, dst = whole[k].at[layer, q, t], part(new[k], k, layer, q, t, whole[k].shape[-1])
-                    pltpu.make_async_copy(src, dst, write.at[k, layer, q, t]).start()
-
-                each(side, put)
-    copies = [pltpu.make_async_copy(src, dst, store.at[i]) for i, (src, dst) in enumerate(zip(state, new_state, strict=True))]
+                if q < COLORS // 2:
+                    c = whole[k].shape[-1]
+                    dst = new[k].at[layer, :, :, q] if k < SLICES - 1 else new[k].at[layer, :, :, :, pl.ds(q * c, c)]
+                    copies.append(pltpu.make_async_copy(whole[k].at[layer, q], dst, write.at[k, layer, q, 0]))
+                else:
+                    for t in range(side):
+                        dst = part(new[k], k, layer, q, t, whole[k].shape[-1])
+                        copies.append(pltpu.make_async_copy(whole[k].at[layer, q, t], dst, write.at[k, layer, q, t]))
+    copies += [pltpu.make_async_copy(src, dst, store.at[i]) for i, (src, dst) in enumerate(zip(state, new_state, strict=True))]
     for copy in copies:
         copy.start()
     for copy in copies:
         copy.wait()
-    for k in range(SLICES):
-        for layer in range(CORES):
-
-            def wrote(i, k=k, layer=layer):
-                q, t = i // side, lax.rem(i, side)
-                pltpu.make_async_copy(whole[k].at[layer, q, t], whole[k].at[layer, q, t], write.at[k, layer, q, t]).wait()
-
-            each(COLORS * side, wrote)
 
 
 def solution(mesh):

time: 243 us -> 241 us (level)
  no operation moved by 1% of the time
where the time goes in v5:
time: 241 us
  Pallas kernels  240 us (100%)
    pallas_call x1, Pallas kernels, step(): pl.pallas_call(functools.partial(step_kernel, side, n, count), name='step...  225 us
    pallas_call x1, Pallas kernels, step(): pl.pallas_call(functools.partial(finish_kernel, side), name='finish', out...  15 us

profile of v5, /device:TPU:97, one launch (start us, length us, event | category | flops | bytes accessed | tf_op | source)
XLA Modules:
  0.0 241.3 jit_solution(2984390272044000541)
XLA Ops:
  0.6 225.5 %step.1 = (bf16[2,4,4,4,16,3200]{5,4,3,2,1,0:T(8,128)(2,1)S(1)}, bf16[2,4,4,4,16,3200]{5,4,3,2,1,0:T(8,128)(2,1)S(1)}, bf16[2,4,4,4,200,256]{5,4,3,2,1,0:T(8,128...) custom-call(bf16[2,4,4,4,16,3200]{5,4,3,2,1,0:T(8,128)(2,1)} %bitcas, ...), custom_call_target="tpu_custom_call" | custom-call | tf_op jit(solution)/shard_map/step/pallas_call | solution.py:549
  226.1 15.0 %finish.1 = (bf16[2,4,4,4,16,3200]{5,4,3,2,1,0:T(8,128)(2,1)}, bf16[2,4,4,4,16,3200]{5,4,3,2,1,0:T(8,128)(2,1)}, bf16[2,4,4,200,1024]{4,3,2,1,0:T(8,128)(2,1)}, ...) custom-call(bf16[2,4,4,4,16,3200]{5,4,3,2,1,0:T(8,128)(2,1)S(1)} %ge, ...), custom_call_target="tpu_custom_call" | custom-call | tf_op jit(solution)/shard_map/finish/pallas_call | solution.py:580

commit v6 on v5

--- a/solution.py
+++ b/solution.py
@@ -495,23 +495,23 @@
 
 def finish_kernel(side, *refs):
     whole, state, new, new_state, write, store = refs[0:3], refs[3:9], refs[9:12], refs[12:18], refs[18], refs[19]
-    copies = []
     for k in range(SLICES):
         for layer in range(CORES):
             for q in range(COLORS):
                 if q < COLORS // 2:
                     c = whole[k].shape[-1]
                     dst = new[k].at[layer, :, :, q] if k < SLICES - 1 else new[k].at[layer, :, :, :, pl.ds(q * c, c)]
-                    copies.append(pltpu.make_async_copy(whole[k].at[layer, q], dst, write.at[k, layer, q, 0]))
+                    pltpu.make_async_copy(whole[k].at[layer, q], dst, write.at[k]).start()
                 else:
                     for t in range(side):
                         dst = part(new[k], k, layer, q, t, whole[k].shape[-1])
-                        copies.append(pltpu.make_async_copy(whole[k].at[layer, q, t], dst, write.at[k, layer, q, t]))
-    copies += [pltpu.make_async_copy(src, dst, store.at[i]) for i, (src, dst) in enumerate(zip(state, new_state, strict=True))]
-    for copy in copies:
-        copy.start()
-    for copy in copies:
-        copy.wait()
+                        pltpu.make_async_copy(whole[k].at[layer, q, t], dst, write.at[k]).start()
+        for i in (k, k + SLICES):
+            pltpu.make_async_copy(state[i], new_state[i], store.at[i]).start()
+    for k in range(SLICES):
+        pltpu.make_async_copy(whole[k], whole[k], write.at[k]).wait()
+    for i in range(2 * SLICES):
+        pltpu.make_async_copy(state[i], new_state[i], store.at[i]).wait()
 
 
 def solution(mesh):
@@ -583,7 +583,7 @@
             out_shape=tuple(shape(a.shape, a.dtype) for a in (*[shape(t.shape, bf16) for t in views], *ms, *vs)),
             in_specs=[VMEM] * 9,
             out_specs=(ANY,) * 9,
-            scratch_shapes=[DMA((SLICES, CORES, COLORS, side)), DMA((2 * SLICES,))],
+            scratch_shapes=[DMA((SLICES,)), DMA((2 * SLICES,))],
             compiler_params=pltpu.CompilerParams(vmem_limit_bytes=22_806_528),
         )(*gathered)
         new = [a.reshape(w.shape) for a, w in zip(outs[:3], weights, strict=True)]

time: 241 us -> 240 us (level)
  no operation moved by 1% of the time
where the time goes in v6:
time: 240 us
  Pallas kernels  240 us (100%)
    pallas_call x1, Pallas kernels, step(): pl.pallas_call(functools.partial(step_kernel, side, n, count), name='step...  225 us
    pallas_call x1, Pallas kernels, step(): pl.pallas_call(functools.partial(finish_kernel, side), name='finish', out...  14.2 us

profile of v6, /device:TPU:97, one launch (start us, length us, event | category | flops | bytes accessed | tf_op | source)
XLA Modules:
  0.0 240.3 jit_solution(9479062511101205572)
XLA Ops:
  0.6 225.5 %step.1 = (bf16[2,4,4,4,16,3200]{5,4,3,2,1,0:T(8,128)(2,1)S(1)}, bf16[2,4,4,4,16,3200]{5,4,3,2,1,0:T(8,128)(2,1)S(1)}, bf16[2,4,4,4,200,256]{5,4,3,2,1,0:T(8,128...) custom-call(bf16[2,4,4,4,16,3200]{5,4,3,2,1,0:T(8,128)(2,1)} %bitcas, ...), custom_call_target="tpu_custom_call" | custom-call | tf_op jit(solution)/shard_map/step/pallas_call | solution.py:549
  226.1 14.2 %finish.1 = (bf16[2,4,4,4,16,3200]{5,4,3,2,1,0:T(8,128)(2,1)}, bf16[2,4,4,4,16,3200]{5,4,3,2,1,0:T(8,128)(2,1)}, bf16[2,4,4,200,1024]{4,3,2,1,0:T(8,128)(2,1)}, ...) custom-call(bf16[2,4,4,4,16,3200]{5,4,3,2,1,0:T(8,128)(2,1)S(1)} %ge, ...), custom_call_target="tpu_custom_call" | custom-call | tf_op jit(solution)/shard_map/finish/pallas_call | solution.py:580
